TPU v7x, 128 devices: a whole 4x4x4 slice. The times are simulated.
128 devices in a mesh: dp: 16 (over z, x), mp: 8 (over y, core).
Axes of the slice: x: 4, y: 4, z: 4, core: 2. Of those that a mesh axis runs over, the one named last changes fastest.
Arguments:
- patches: bfloat16 [24576, 1280], P('dp', 'mp'), may hold values from -6 to 6
- cotangent: bfloat16 [24576, 1280], P('dp', 'mp'), may hold values from -0.29882812 to 0.29882812
- encoder_rank: int32 [192], P('dp'), may hold values from 0 to 15, as said below
- block_fill: int32 [192], P('dp'), may hold values from 32 to 128
- w_up: bfloat16 [1280, 5120], P(None, 'mp'), may hold values from -0.15625 to 0.15625
- w_down: bfloat16 [5120, 1280], P('mp'), may hold values from -0.078125 to 0.078125
- q_up: float32 [5120, 64], P('mp'), may hold values from -6 to 6
- q_down: float32 [1280, 64], replicated, may hold values from -6 to 6
Outputs:
- encoded: bfloat16 [36864, 1280], P('dp', 'mp')
- approx_up: float32 [1280, 5120], P(None, 'mp')
- approx_down: float32 [5120, 1280], P('mp')
- qnew_up: float32 [5120, 64], P('mp')
- qnew_down: float32 [1280, 64], replicated
Inputs may be any that keep to these rules, and one draw needn't show every extreme that they name: `encoder_rank`: from the blocks of one data rank at most 2 go to one encoder rank, and one encoder rank receives at most 18 blocks in all; both bounds are reached in every draw. Every encoder rank receives some block.
All inputs are finite; a program needn't handle non-finite values.
Results may differ from a plain program's by a relative error of at most 0.015.
Values may be sent and summed in bfloat16 or wider, within the bound.
A program may use at most 128 MiB of HBM per device.

v0:
```python
import jax
import jax.numpy as jnp
from jax import lax
from jax.sharding import Mesh
from jax.sharding import PartitionSpec as P

BLOCK = 128
CAP = 2
DP = ("dp_0", "dp_1")
MP = ("mp_0", "mp_1")
DP_MP = ("dp_0", "dp_1", "mp_0", "mp_1")


def rows_first(arrays, axis, dims):
    turned = [jnp.moveaxis(a, dim, 0) for a, dim in zip(arrays, dims)]
    both = jnp.concatenate([t.reshape(len(t), -1) for t in turned], axis=1)
    whole, at, done = (lax.all_gather(both, axis, axis=0, tiled=True), 0, [])
    for t, dim in zip(turned, dims):
        share = whole[:, at : at + t[0].size].reshape(-1, *t.shape[1:])
        done.append(jnp.moveaxis(share, 0, dim))
        at += t[0].size
    return tuple(done)


def rows_for(lines, count):
    spare = -len(lines) % count
    return jnp.pad(lines, [(0, spare)] + [(0, 0)] * (lines.ndim - 1))


def own_block(blocks, axes, order):
    shape = [lax.axis_size(a) for a in axes]
    blocks = blocks.reshape(*shape, *blocks.shape[1:])
    blocks = blocks.transpose(*order, *range(len(axes), blocks.ndim))
    blocks = blocks.reshape(-1, *blocks.shape[len(axes) :])
    for k in order:
        blocks = lax.psum_scatter(blocks, axes[k], scatter_dimension=0, tiled=True)
    return blocks[0]


def all_blocks(shard, axes, order):
    blocks = shard[None]
    for k in order:
        blocks = lax.all_gather(blocks, axes[k], axis=0, tiled=True)
    held = [lax.axis_size(axes[k]) for k in reversed(order)]
    blocks = blocks.reshape(*held, *shard.shape)
    turned = sorted(range(len(order)), key=lambda place: order[len(order) - 1 - place])
    return blocks.transpose(*turned, *range(len(order), blocks.ndim)).reshape(-1, *shard.shape)


def total_of(shard, axes, order):
    count, lines = (lax.axis_size(axes), shard.reshape(-1, *shard.shape[1:][-1:]))
    blocks = rows_for(lines, count).reshape(count, -1, *lines.shape[1:])
    own = own_block(blocks, axes, order)
    whole = all_blocks(own, axes, order[::-1]).reshape(-1, *lines.shape[1:])
    return whole[: len(lines)].reshape(shard.shape)


def copy_for_each(shard, axis):
    count = lax.axis_size(axis)
    return lax.all_to_all(
        jnp.broadcast_to(shard[None], (count, *shard.shape)), axis, 0, 0, tiled=True
    )


def of_everyone(shard, axis):
    everything = copy_for_each(shard, axis)
    return jnp.sum(everything, axis=0)


def over_copies(shard, axis):
    return copy_for_each(shard, axis).astype(jnp.float32).sum(axis=0)


def over_axes(shard, axes):
    for axis in axes:
        shard = lax.psum(shard, axis)
    return shard


def gelu_parts(preact):
    sig = jax.nn.sigmoid(1.702 * preact)
    return (preact * sig, sig + 1.702 * preact * sig * (1.0 - sig))


def row_keep(fills):
    within = jnp.arange(BLOCK, dtype=jnp.int32)
    return (within[None, :] < fills[:, None]).reshape(-1, 1)


def send_plan(enc_ranks, block_fills, destinations):
    total_blocks = enc_ranks.shape[0]
    block_ids = jnp.arange(total_blocks, dtype=jnp.int32)
    before = (enc_ranks[None, :] == enc_ranks[:, None]) & (block_ids[None, :] < block_ids[:, None])
    ordinal = jnp.sum(before.astype(jnp.int32), axis=1)
    target = enc_ranks * CAP + ordinal
    places = jnp.arange(destinations * CAP, dtype=jnp.int32)
    chosen = places[:, None] == target[None, :]
    slot_fill = jnp.sum(jnp.where(chosen, block_fills[None, :], 0), axis=1)
    return (chosen.astype(jnp.bfloat16), slot_fill.reshape(destinations, CAP))


def compact_plan(recv_fill, most_blocks):
    flat_fill = recv_fill.reshape(-1)
    occupied = flat_fill > 0
    position = jnp.cumsum(occupied.astype(jnp.int32)) - 1
    targets = jnp.arange(most_blocks, dtype=jnp.int32)
    picked = occupied[None, :] & (position[None, :] == targets[:, None])
    kept_fill = jnp.sum(jnp.where(picked, flat_fill[None, :], 0), axis=1).astype(jnp.int32)
    return (picked.astype(jnp.bfloat16), kept_fill)


def select_rows(selector, blocks_in):
    flat_rows = blocks_in.reshape(selector.shape[1], -1)
    return jnp.dot(selector, flat_rows, preferred_element_type=jnp.float32).astype(jnp.bfloat16)


def local_layer(patches_full, cot_full, fills, w_up, w_down):
    keep_rows = row_keep(fills)
    preact = jnp.dot(patches_full, w_up, preferred_element_type=jnp.float32)
    active, slope = gelu_parts(preact)
    hidden = active.astype(jnp.bfloat16)
    partial_rows = jnp.where(
        keep_rows, jnp.dot(hidden, w_down, preferred_element_type=jnp.float32), 0.0
    )
    masked_cot = jnp.where(keep_rows, cot_full, jnp.zeros((), jnp.bfloat16))
    grad_hidden = lax.dot_general(
        masked_cot, w_down, (((1,), (1,)), ((), ())), preferred_element_type=jnp.float32
    )
    grad_pre = (grad_hidden * slope).astype(jnp.bfloat16)
    grad_up = lax.dot_general(
        patches_full, grad_pre, (((0,), (0,)), ((), ())), preferred_element_type=jnp.float32
    )
    grad_down = lax.dot_general(
        hidden, masked_cot, (((0,), (0,)), ((), ())), preferred_element_type=jnp.float32
    )
    return (partial_rows, grad_up, grad_down)


def orthonormal(proj, gram):
    lower = jnp.linalg.cholesky(gram)
    return jax.scipy.linalg.solve_triangular(lower, proj.T, lower=True).T


def local(patches, cotangent, encoder_rank, block_fill, w_up, w_down, q_up, q_down):
    ranks_dp = lax.axis_size(DP)
    total_blocks = encoder_rank.shape[0]
    most_blocks = total_blocks + 6
    features = patches.shape[1]
    chosen, slot_fill = send_plan(encoder_rank, block_fill, ranks_dp)
    full_in, full_cot = rows_first((patches, cotangent), MP, (1, 1))
    partial_rows, grad_up, grad_down = local_layer(full_in, full_cot, block_fill, w_up, w_down)
    own_out = lax.psum_scatter(partial_rows, MP, scatter_dimension=1, tiled=True).astype(
        jnp.bfloat16
    )
    send_out = select_rows(chosen, own_out.reshape(total_blocks, -1)).reshape(ranks_dp, CAP, -1)
    recv_out, recv_fill = (
        lax.all_to_all(send_out, DP, split_axis=0, concat_axis=0, tiled=True),
        lax.all_to_all(slot_fill, DP, split_axis=0, concat_axis=0, tiled=True),
    )
    picked, kept_fill = compact_plan(recv_fill, most_blocks)
    encoded = select_rows(picked, recv_out).reshape(-1, features)
    proj_up_part = jnp.dot(grad_up, q_up)
    proj_down_part = jnp.dot(grad_down, q_down)
    proj_up = total_of(proj_up_part, DP_MP, (0, 1, 2, 3))
    proj_down = of_everyone(proj_down_part, DP)
    gram_down = of_everyone(jnp.dot(proj_down.T, proj_down), MP)
    basis_up = orthonormal(proj_up, jnp.dot(proj_up.T, proj_up))
    basis_down = orthonormal(proj_down, gram_down)
    fresh_up_part = lax.dot_general(grad_up, basis_up, (((0,), (0,)), ((), ())))
    fresh_down_part = lax.dot_general(grad_down, basis_down, (((0,), (0,)), ((), ())))
    fresh_up = over_copies(fresh_up_part.astype(jnp.bfloat16), DP).astype(jnp.float32)
    fresh_down = over_axes(fresh_down_part, DP_MP)
    approx_up = jnp.dot(basis_up, fresh_up.T)
    approx_down = jnp.dot(basis_down, fresh_down.T)
    return (encoded, approx_up, approx_down, fresh_up, fresh_down)


def solution(mesh):
    torus = Mesh(mesh.devices.reshape(4, 4, 4, 2), ("dp_0", "dp_1", "mp_0", "mp_1"))
    in_specs = (P(DP, MP), P(DP, MP), P(DP), P(DP), P(None, MP), P(MP, None), P(MP, None), P())
    out_specs = (P(DP, MP), P(None, MP), P(MP, None), P(MP, None), P())
    return jax.shard_map(local, mesh=torus, in_specs=in_specs, out_specs=out_specs, check_vma=False)
```

profile of v0, /device:TPU:1, one launch (start us, length us, event | category | flops | bytes accessed | tf_op | source)
XLA Modules:
  0.0 399.4 jit_solution(5153608027994693691)
XLA Ops:
  10.3 51.1 %all-gather.2.cloned.1.call-done = bf16[1280,3072]{1,0:T(8,128)(2,1)} async-done(((bf16[160,3072]{1,0:T(8,128)(2,1)}), bf16[1280,3072]{1,0:T(8,128)(2,1)}) %all-gather.2.cloned.1.call-update) | async-done | bytes 7864336 | tf_op jit(solution)/shard_map/all_gather | solution.py:17
  61.4 6.1 %fusion.2 = f32[1536,640]{1,0:T(8,128)S(1)} fusion(bf16[1280,640]{1,0:T(8,128)(2,1)} %param.13, bf16[1280,3072]{1,0:T(8,128)(2,1)} %all-gather.2.cloned.1.call-done), kind=kOutput, calls=%fused_computation.9 | convolution fusion | flops 2516582400 | bytes 9502720 | tf_op jit(solution)/shard_map/dot_general | solution.py:119
  67.5 3.6 fusion.4
  73.5 6.7 %all-to-all-start.3 = ((f32[16,640,64]{1,2,0:T(8,128)}), f32[16,640,64]{1,2,0:T(8,128)}, u32[]{:S(2)}, u32[]{:S(2)}) async-start(f32[16,640,64]{1,2,0:T(8,128)} %broadcast_in_dim.74), calls=%async_computation.6 | async-start | bytes 5242880 | tf_op jit(solution)/shard_map/all_to_all | solution.py:60
  80.5 11.1 %fusion = bf16[1280,640]{1,0:T(8,128)(2,1)S(1)} fusion(bf16[1280,3072]{1,0:T(8,128)(2,1)} %all-gather.2.cloned.1.call-done, f32[1536,640]{1,0:T(8,128)} %copy-done.12, bf16[640,1280]{1,0:T(8,128)(2,1)S(1)} %copy-done, pred[1536]{0:T(1024)(128)(4,1)S(1)} %fusion.22), kind=kOutput, calls=%fused_computation.7 | convolution fusion | flops 5044961280 | bytes 15074816 | tf_op jit(solution)/shard_map/dot_general | solution.py:130
  95.2 25.3 %all-to-all-done.3 = f32[16,640,64]{1,2,0:T(8,128)} async-done(((f32[16,640,64]{1,2,0:T(8,128)}), f32[16,640,64]{1,2,0:T(8,128)}, u32[]{:S(2)}, u32[]{:S(2)}) %all-to-all-start.3) | async-done | bytes 2621472 | tf_op jit(solution)/shard_map/all_to_all | solution.py:60
  125.0 5.3 %all-to-all-start.4 = ((f32[8,1,4096]{2,1,0:T(1,128)}), f32[8,1,4096]{2,1,0:T(1,128)}, u32[]{:S(2)}, u32[]{:S(2)}) async-start(f32[8,1,4096]{2,1,0:T(1,128)} %reshape.134), calls=%async_computation.7 | async-start | bytes 262144 | tf_op jit(solution)/shard_map/all_to_all | solution.py:60
  131.1 4.6 %all-to-all-done.4 = f32[8,1,4096]{2,1,0:T(1,128)} async-done(((f32[8,1,4096]{2,1,0:T(1,128)}), f32[8,1,4096]{2,1,0:T(1,128)}, u32[]{:S(2)}, u32[]{:S(2)}) %all-to-all-start.4) | async-done | bytes 131104 | tf_op jit(solution)/shard_map/all_to_all | solution.py:60
  141.6 5.8 %cholesky.55 = f32[64,64]{1,0:T(8,128)S(1)} custom-call(f32[64,64]{1,0:T(8,128)S(1)} %fusion.14), custom_call_target="Cholesky" | custom-call | tf_op jit(solution)/shard_map/jit(cholesky)/cholesky | solution.py:140
  148.7 4.9 %custom-call.11 = f32[1,64,64]{1,2,0:T(8,128)S(1)} custom-call(f32[1,64,64]{2,1,0:T(8,128)S(1)} %fusion.11), custom_call_target="InvertDiagBlocksLowerTriangular" | custom-call | tf_op jit(solution)/shard_map/jit(_solve_triangular)/triangular_solve | solution.py:141
  156.9 7.7 %convolution_select_fusion = f32[1536,1280]{0,1:T(8,128)} fusion(bf16[640,1280]{1,0:T(8,128)(2,1)S(1)} %copy-done, pred[1536]{0:T(1024)(128)(4,1)} %copy-done.6, f32[1536,640]{1,0:T(8,128)} %copy-done.12), kind=kOutput, calls=%fused_computation.2 | convolution fusion | flops 2524446720 | bytes 13436416 | tf_op jit(solution)/shard_map/dot_general | solution.py:123
  166.2 3.9 all-to-all-start
  172.8 12.5 %all-reduce = f32[8,10,64]{2,0,1:T(8,128)S(1)} all-reduce(f32[8,10,64]{2,0,1:T(8,128)S(1)} %copy.56), channel_id=5, replica_groups=mesh['dp_0'=4,'dp_1'=4,'mp_0'=4,'mp_1'=2] {'mp_0'}, use_global_device_ids=true, to_apply=%region_6.7.clone | all-reduce | flops 5120 | bytes 40960
  185.4 7.5 %all-reduce.1 = f32[2,10,64]{2,0,1:T(2,128)S(1)} all-reduce(f32[2,10,64]{2,0,1:T(2,128)S(1)} %constant_dynamic-slice_fusion.1), channel_id=6, replica_groups=mesh['dp_0'=4,'dp_1'=4,'mp_0'=4,'mp_1'=2] {'mp_1'}, use_global_device_ids=true, to_apply=%region_7.8.clone | all-reduce | flops 1280 | bytes 10240
  195.4 9.0 %all_gather.17 = f32[8,10,64]{2,1,0:T(8,128)S(1)} all-gather(f32[2,10,64]{2,1,0:T(8,128)S(1)} %all_gather.16), channel_id=1, replica_groups=mesh['dp_0'=4,'dp_1'=4,'mp_0'=4,'mp_1'=2] {'mp_0'}, dimensions={0}, use_global_device_ids=true | all-gather | bytes 25600 | tf_op jit(solution)/shard_map/all_gather | solution.py:43
  204.3 10.3 %all_gather.18 = f32[32,10,64]{2,0,1:T(8,128)S(1)} all-gather(f32[8,10,64]{2,0,1:T(8,128)S(1)} %copy.58), channel_id=1, replica_groups=mesh['dp_0'=4,'dp_1'=4,'mp_0'=4,'mp_1'=2] {'dp_1'}, dimensions={0}, use_global_device_ids=true | all-gather | bytes 102400 | tf_op jit(solution)/shard_map/all_gather | solution.py:43
  214.7 12.3 %all_gather.19 = f32[128,10,64]{2,0,1:T(8,128)S(1)} all-gather(f32[32,10,64]{2,0,1:T(8,128)S(1)} %all_gather.18), channel_id=1, replica_groups=mesh['dp_0'=4,'dp_1'=4,'mp_0'=4,'mp_1'=2] {'dp_0'}, dimensions={0}, use_global_device_ids=true | all-gather | bytes 409600 | tf_op jit(solution)/shard_map/all_gather | solution.py:43
  228.7 5.8 %cholesky.44 = f32[64,64]{1,0:T(8,128)S(1)} custom-call(f32[64,64]{1,0:T(8,128)S(1)} %fusion.17), custom_call_target="Cholesky" | custom-call | tf_op jit(solution)/shard_map/jit(cholesky)/cholesky | solution.py:140
  235.8 5.5 %custom-call.10 = f32[1,64,64]{1,2,0:T(8,128)} custom-call(f32[1,64,64]{2,1,0:T(8,128)S(1)} %fusion.10), custom_call_target="InvertDiagBlocksLowerTriangular" | custom-call | tf_op jit(solution)/shard_map/jit(_solve_triangular)/triangular_solve | solution.py:141
  248.6 5.8 %all-to-all-start.2 = ((bf16[16,640,64]{1,2,0:T(8,128)(2,1)}), bf16[16,640,64]{1,2,0:T(8,128)(2,1)S(1)}, u32[]{:S(2)}, u32[]{:S(2)}) async-start(bf16[16,640,64]{1,2,0:T(8,128)(2,1)} %broadcast_in_dim.49), calls=%async_computation.5 | async-start | bytes 2621440 | tf_op jit(solution)/shard_map/all_to_all | solution.py:60
  269.0 5.7 %all-to-all-start.1 = ((bf16[16,2,20480]{2,1,0:T(2,128)(2,1)}), bf16[16,2,20480]{2,1,0:T(2,128)(2,1)}, u32[]{:S(2)}, u32[]{:S(2)}) async-start(bf16[16,2,20480]{2,1,0:T(2,128)(2,1)} %reshape.113), calls=%async_computation.2 | async-start | bytes 2621440 | tf_op jit(solution)/shard_map/all_to_all | solution.py:157
  274.7 32.4 %all-reduce.9.cloned.1.call-done = f32[1280,64]{0,1:T(8,128)} async-done(((f32[1280,64]{0,1:T(8,128)}), f32[1280,64]{0,1:T(8,128)}) %all-reduce.9.cloned.1.call-update) | async-done | bytes 327696 | tf_op jit(solution)/shard_map/psum | solution.py:76
  307.9 44.2 %all-reduce.11.cloned.1.call-done = f32[1280,64]{0,1:T(8,128)} async-done(((f32[1280,64]{0,1:T(8,128)}), f32[1280,64]{0,1:T(8,128)}) %all-reduce.11.cloned.1.call-update) | async-done | bytes 327696 | tf_op jit(solution)/shard_map/psum | solution.py:76
  354.7 26.9 %all-reduce.13.cloned.1.call-done = f32[1280,64]{0,1:T(8,128)} async-done(((f32[1280,64]{0,1:T(8,128)}), f32[1280,64]{0,1:T(8,128)}) %all-reduce.13.cloned.1.call-update) | async-done | bytes 327696 | tf_op jit(solution)/shard_map/psum | solution.py:76
  (112 shorter events, 70.2 us)
Async XLA Ops:
  7.2 73.3 %copy-start = (bf16[640,1280]{1,0:T(8,128)(2,1)S(1)}, bf16[640,1280]{1,0:T(8,128)(2,1)}, u32[]{:S(2)}) copy-start(bf16[640,1280]{1,0:T(8,128)(2,1)} %param.14) | copy-start | bytes 4915204
  7.2 54.2 %all-gather.2.cloned.1.call-start = ((), (), s32[]{:S(2)}) async-start(), calls=%async_computation.8 | async-start | bytes 8847360 | tf_op jit(solution)/shard_map/all_gather | solution.py:17
  10.3 70.2 %copy-start.6 = (pred[1536]{0:T(1024)(128)(4,1)}, pred[1536]{0:T(1024)(128)(4,1)S(1)}, u32[]{:S(2)}) copy-start(pred[1536]{0:T(1024)(128)(4,1)S(1)} %fusion.22) | copy-start | bytes 4612
  61.4 6.1 %copy-start.8 = (bf16[1280,3072]{1,0:T(8,128)(2,1)S(1)}, bf16[1280,3072]{1,0:T(8,128)(2,1)}, u32[]{:S(2)}) copy-start(bf16[1280,3072]{1,0:T(8,128)(2,1)} %all-gather.2.cloned.1.call-done) | copy-start | bytes 23592964
  67.5 3.6 copy-start.12
  67.5 3.6 copy-start.4
  71.1 9.1 %copy-start.1 = (bf16[640,1280]{1,0:T(8,128)(2,1)}, bf16[640,1280]{1,0:T(8,128)(2,1)S(1)}, u32[]{:S(2)}) copy-start(bf16[640,1280]{1,0:T(8,128)(2,1)S(1)} %fusion.4) | copy-start | bytes 4915204
  73.5 47.0 %all-to-all-start.3 = ((f32[16,640,64]{1,2,0:T(8,128)}), f32[16,640,64]{1,2,0:T(8,128)}, u32[]{:S(2)}, u32[]{:S(2)}) async-start(f32[16,640,64]{1,2,0:T(8,128)} %broadcast_in_dim.74), calls=%async_computation.6 | async-start | bytes 5242880 | tf_op jit(solution)/shard_map/all_to_all | solution.py:60
  80.2 11.4 %copy-start.5 = (f32[640,64]{0,1:T(8,128)S(1)}, f32[640,64]{0,1:T(8,128)}, u32[]{:S(2)}) copy-start(f32[640,64]{0,1:T(8,128)} %param.15) | copy-start | bytes 491524
  80.3 50.1 %reduce-scatter.8.cloned.1.call-start = ((), (), s32[]{:S(2)}) async-start(), calls=%async_computation.10 | async-start | bytes 1310720 | tf_op jit(solution)/shard_map/reduce_scatter | solution.py:36
  125.0 10.7 %all-to-all-start.4 = ((f32[8,1,4096]{2,1,0:T(1,128)}), f32[8,1,4096]{2,1,0:T(1,128)}, u32[]{:S(2)}, u32[]{:S(2)}) async-start(f32[8,1,4096]{2,1,0:T(1,128)} %reshape.134), calls=%async_computation.7 | async-start | bytes 262144 | tf_op jit(solution)/shard_map/all_to_all | solution.py:60
  130.4 41.5 %reduce-scatter.10.cloned.1.call-start = ((), (), s32[]{:S(2)}) async-start(), calls=%async_computation.11 | async-start | bytes 327680 | tf_op jit(solution)/shard_map/reduce_scatter | solution.py:36
  131.1 123.3 %all-reduce.7.cloned.1.call-start = ((), (), s32[]{:S(2)}) async-start(), calls=%async_computation.12 | async-start | bytes 655360 | tf_op jit(solution)/shard_map/psum | solution.py:76
  156.6 98.4 %reduce-scatter.6.cloned.1.call-start = ((), (), s32[]{:S(2)}) async-start(), calls=%async_computation.9 | async-start | bytes 8847360 | tf_op jit(solution)/shard_map/reduce_scatter | solution.py:152
  164.5 5.5 %copy-start.11 = (u32[128]{0:T(128)S(1)}, u32[128]{0:T(128)}, u32[]{:S(2)}) copy-start(u32[128]{0:T(128)} %constant.61) | copy-start | bytes 1540
  164.5 6.1 %copy-start.10 = (u32[128]{0:T(128)S(1)}, u32[128]{0:T(128)}, u32[]{:S(2)}) copy-start(u32[128]{0:T(128)} %constant.65) | copy-start | bytes 1540
  166.2 80.3 %all-to-all-start = ((s32[16,1,2]{2,1,0:T(1,128)}), s32[16,1,2]{2,1,0:T(1,128)S(1)}, u32[]{:S(2)}, u32[]{:S(2)}) async-start(s32[16,1,2]{2,1,0:T(1,128)} %bitcast), calls=%async_computation | async-start | bytes 16384 | tf_op jit(solution)/shard_map/all_to_all | solution.py:158
  248.6 20.4 %all-to-all-start.2 = ((bf16[16,640,64]{1,2,0:T(8,128)(2,1)}), bf16[16,640,64]{1,2,0:T(8,128)(2,1)S(1)}, u32[]{:S(2)}, u32[]{:S(2)}) async-start(bf16[16,640,64]{1,2,0:T(8,128)(2,1)} %broadcast_in_dim.49), calls=%async_computation.5 | async-start | bytes 2621440 | tf_op jit(solution)/shard_map/all_to_all | solution.py:60
  254.4 52.8 %all-reduce.9.cloned.1.call-start = ((), (), s32[]{:S(2)}) async-start(), calls=%async_computation.13 | async-start | bytes 655360 | tf_op jit(solution)/shard_map/psum | solution.py:76
  269.0 115.8 %all-to-all-start.1 = ((bf16[16,2,20480]{2,1,0:T(2,128)(2,1)}), bf16[16,2,20480]{2,1,0:T(2,128)(2,1)}, u32[]{:S(2)}, u32[]{:S(2)}) async-start(bf16[16,2,20480]{2,1,0:T(2,128)(2,1)} %reshape.113), calls=%async_computation.2 | async-start | bytes 2621440 | tf_op jit(solution)/shard_map/all_to_all | solution.py:157
  274.7 77.4 %all-reduce.11.cloned.1.call-start = ((), (), s32[]{:S(2)}) async-start(), calls=%async_computation.14 | async-start | bytes 655360 | tf_op jit(solution)/shard_map/psum | solution.py:76
  307.2 74.3 %all-reduce.13.cloned.1.call-start = ((), (), s32[]{:S(2)}) async-start(), calls=%async_computation.15 | async-start | bytes 655360 | tf_op jit(solution)/shard_map/psum | solution.py:76
  352.3 29.2 %copy-start.3 = (f32[640,64]{0,1:T(8,128)}, f32[640,64]{0,1:T(8,128)S(1)}, u32[]{:S(2)}) copy-start(f32[640,64]{0,1:T(8,128)S(1)} %convert_reduce_fusion) | copy-start | bytes 491524
  384.8 7.0 %copy-start.2 = (f32[1280,64]{0,1:T(8,128)S(1)}, f32[1280,64]{0,1:T(8,128)}, u32[]{:S(2)}) copy-start(f32[1280,64]{0,1:T(8,128)} %all-reduce.13.cloned.1.call-done) | copy-start | bytes 983044
  (2 other events, 1.5 us)
Sparse Core Ops, SparseCore 0:
  10.3 51.0 all-gather.1
  95.3 30.8 reduce-scatter.7
  133.5 17.0 reduce-scatter.9
  156.7 38.9 all-reduce.6
  198.0 51.9 reduce-scatter.5
  257.2 49.9 all-reduce.8
  309.5 42.5 all-reduce.10
  354.6 26.9 all-reduce.12
where the time goes:
time: 401 us; the launch traced here: 399 us
  waiting for transfers between devices  187 us (47%)
  blocking collectives  53.4 us (13%)
  matrix products  46.6 us (12%)
  other arithmetic  35.9 us (9%)
  local copies, waits for them, and re-layouts  33.2 us (8%)
  starting transfers between devices  28.3 us (7%)
  between operations  15.1 us (4%)
    psum x4, waiting for transfers between devices, over_axes(): shard = lax.psum(shard, axis)  104 us
    all_gather x1, waiting for transfers between devices, rows_first(): whole, at, done = (lax.all_gather(both, axis, axis=0, tiled=True), 0, [])  51.1 us
    all_gather x4, blocking collectives, all_blocks(): blocks = lax.all_gather(blocks, axes[k], axis=0, tiled=True)  33.4 us
    all_to_all x3, waiting for transfers between devices, copy_for_each(): lax.all_to_all(jnp.broadcast_to(shard[None], (count, *shard.shape)), axis...  30.9 us
    unnamed x2, blocking collectives  20.1 us
    all_to_all x3, starting transfers between devices, copy_for_each(): lax.all_to_all(jnp.broadcast_to(shard[None], (count, *shard.shape)), axis...  17.8 us
    another operation x6, other arithmetic, orthonormal(): lower = jnp.linalg.cholesky(gram)  13 us
    another operation x4, other arithmetic, orthonormal(): return jax.scipy.linalg.solve_triangular(lower, proj.T, lower=True).T  11.7 us
  transfers between devices with their start and end apart: 13, of which 7 were waited for; matrix products, arithmetic and copies ran while one was open for 23% of the time, Pallas kernels for 0%

commit v1 on v0

v1 whole, which is shorter than its diff:
```python
import jax
import jax.numpy as jnp
from jax import lax
from jax.experimental import pallas as pl
from jax.experimental.pallas import tpu as pltpu
from jax.sharding import PartitionSpec as P

BLOCK = 128
CAP = 2
RMAX = 18
N_DP = 16
N_Y = 4
N_MP = 8
RANK = 64
NC = 6
HALF = NC // 2
AHEAD = 2
MESH = pl.DeviceIdType.MESH
F32 = jnp.float32
BF16 = jnp.bfloat16
NT = (((1,), (1,)), ((), ()))
TN = (((0,), (0,)), ((), ()))


def mm(a, b):
    return jnp.dot(a, b, preferred_element_type=F32)


def mm_nt(a, b):
    return lax.dot_general(a, b, NT, preferred_element_type=F32)


def mm_tn(a, b):
    return lax.dot_general(a, b, TN, preferred_element_type=F32)


def parts(v):
    hi = v.astype(BF16)
    lo = (v - hi.astype(F32)).astype(BF16)
    return hi, lo


def stack2(v):
    return jnp.concatenate(parts(v), axis=0)


def fold2(v):
    return v[:RANK] + v[RANK:]


def left3(v):
    hi, lo = parts(v)
    return jnp.concatenate([hi, hi, lo], axis=0)


def right3(v):
    hi, lo = parts(v)
    return jnp.concatenate([hi, lo, hi], axis=0)


def gram_of(v):
    s = stack2(v)
    g = mm_nt(s, s)
    return g[:RANK, :RANK] + g[:RANK, RANK:] + g[RANK:, :RANK] + g[RANK:, RANK:]


def inverse_factors(grams):
    n = RANK
    row = lax.broadcasted_iota(jnp.int32, (2, n, 2 * n), 1)
    lane = lax.broadcasted_iota(jnp.int32, (2, n, 2 * n), 2)
    eye = jnp.where(lane == row + n, 1.0, 0.0).astype(F32)
    w = jnp.concatenate([grams, jnp.zeros_like(grams)], axis=2) + eye
    for k in range(n - 1):
        pivot = w[:, k : k + 1, k : k + 1]
        line = w[:, k : k + 1, :] * (1.0 / pivot)
        column = w[:, :, k : k + 1]
        w = w - jnp.where(row > k, column * line, 0.0)
    diag = jnp.sum(jnp.where(lane == row, w, 0.0), axis=2, keepdims=True)
    return (w * lax.rsqrt(diag))[:, :, n:]


def kernel_body(
    slot_idx, xin, cin, wu, wd, qu, qd, er, keep,
    a2o, era_out, a3u, b3u, a3d, b3d, qnu, qnd,
    xall, call, hid, gp, wut, wdt, quh, qdh,
    proj, small, pbuf, rsb, rcv, ysend, ybuf, agb, bigf,
    gbuf, outp, po, osb, ra, rb, da, db, fa, fb, ea, eb, ob, a2s, a2r, erb,
    gs, gr, os_, or_, ys, yr, ars, arr, gms, gmr, ers, err_, a2ss, a2rr,
):
    dp = lax.axis_index("dp")
    mp = lax.axis_index("mp")
    y = mp // 2
    c = mp % 2
    right = ((y + 1) % N_Y) * 2 + c
    left = ((y + 3) % N_Y) * 2 + c
    far = ((y + 2) % N_Y) * 2 + c
    mate = y * 2 + (1 - c)
    feats = xin.shape[1]
    tc = xin.shape[2]
    half = proj.shape[3]

    def send(src, dst, ssem, rsem, dpi, mpi):
        return pltpu.make_async_remote_copy(
            src_ref=src, dst_ref=dst, send_sem=ssem, recv_sem=rsem,
            device_id=(dpi, mpi), device_id_type=MESH,
        )

    def dp_at(t):
        return (dp + t) % N_DP

    def mp_at(t):
        return (mp + t) % N_MP

    barrier = pltpu.get_barrier_semaphore()
    for t in range(1, N_DP):
        pl.semaphore_signal(barrier, inc=1, device_id=(dp_at(t), mp), device_id_type=MESH)
    for t in range(1, N_MP):
        pl.semaphore_signal(barrier, inc=1, device_id=(dp, mp_at(t)), device_id_type=MESH)
    pl.semaphore_wait(barrier, N_DP + N_MP - 2)

    def rows(ref, i, owner):
        return ref.at[i, pl.ds(pl.multiple_of(owner * feats, 32), feats), :]

    def own_copy(i, slot):
        src, all_, to = {
            0: (xin, xall, right), 1: (cin, call, left), 2: (cin, call, right),
            3: (xin, xall, left), 6: (xin, xall, mate), 7: (cin, call, mate),
        }[slot]
        return send(src.at[i], rows(all_, i, mp), gs.at[i, slot], gr.at[i, slot], dp, to)

    def pass_copy(i, slot):
        all_, owner, to = {
            4: (xall, left, right), 5: (call, right, left),
            8: (xall, left, mate), 9: (call, right, mate), 10: (call, left, mate),
            11: (xall, right, mate), 12: (xall, far, mate), 13: (call, far, mate),
        }[slot]
        return send(rows(all_, i, owner), rows(all_, i, owner), gs.at[i, slot], gr.at[i, slot], dp, to)

    def start_own(i):
        for slot in (0, 1, 2, 3):
            own_copy(i, slot).start()

    def start_mate(i):
        for slot in (6, 7):
            own_copy(i, slot).start()

    def got(i, slot):
        (own_copy if slot in (0, 1, 2, 3, 6, 7) else pass_copy)(i, slot).wait_recv()

    for i in range(AHEAD):
        start_own(i)
    for i in range(NC):
        start_mate(i)
    for t in range(1, N_DP):
        send(er, erb.at[dp], ers.at[t], err_.at[t], dp_at(t), mp).start()

    erb[dp] = er[...]
    for i in range(NC):
        xall[i, pl.ds(pl.multiple_of(mp * feats, 32), feats), :] = xin[i]
        call[i, pl.ds(pl.multiple_of(mp * feats, 32), feats), :] = cin[i]
    ff = wu.shape[1]
    for j in range(ff // 128):
        wut[j * 128 : (j + 1) * 128, :] = wu[:, j * 128 : (j + 1) * 128].T
    for j in range(wd.shape[1] // 128):
        wdt[j * 128 : (j + 1) * 128, :] = wd[:, j * 128 : (j + 1) * 128].T
    quh[...] = stack2(qu[...])
    qdh[...] = stack2(qd[...])
    proj[0] = jnp.zeros_like(proj[0])
    small[0] = jnp.zeros_like(small[0])
    proj[1] = jnp.zeros_like(proj[1])
    small[1] = jnp.zeros_like(small[1])

    def out_copy(i):
        return send(outp.at[i, 1 - c], po.at[i], os_.at[i], or_.at[i], dp, mate)

    def out_sum(i):
        out_copy(i).wait_recv()
        osb[i] = (outp[i, c].astype(F32) + po[i].astype(F32)).astype(BF16)

    def work_a(i):
        pre = mm(wut[...], xall[i])
        grad = mm(wd[...], call[i])
        sig = jax.nn.sigmoid(1.702 * pre)
        act = pre * sig
        hid[i] = act.astype(BF16)
        gp[i] = (grad * (sig + 1.702 * act * (1.0 - sig))).astype(BF16)

    def work_b(i):
        o = mm(wdt[...], hid[i]).astype(BF16)
        for m in range(N_MP):
            at = (m // 2) * feats
            outp[i, m % 2, at : at + feats, :] = o[m * feats : (m + 1) * feats]
        out_copy(i).start()

    def add_projection(ph, i, left_u, left_d):
        if ph == 0:
            t = fold2(mm(left_u, gp[i]))
            u = fold2(mm(left_d, call[i]))
            big_rhs, small_rhs = xall[i], hid[i]
        else:
            u = fold2(mm(left_u, xall[i]))
            t = fold2(mm(left_d, hid[i]))
            big_rhs, small_rhs = call[i], gp[i]
        big = fold2(mm_nt(stack2(t), big_rhs))
        proj[ph, 0] += big[:, :half]
        proj[ph, 1] += big[:, half:]
        small[ph] += fold2(mm_nt(stack2(u), small_rhs))

    def step(i, carry):
        @pl.when(i < NC)
        def _():
            got(i, 0)
            got(i, 1)
            pass_copy(i, 4).start()
            pass_copy(i, 5).start()
            pass_copy(i, 8).start()
            pass_copy(i, 9).start()

            @pl.when(i + AHEAD < NC)
            def _():
                start_own(i + AHEAD)

        @pl.when(i > 0)
        def _():
            work_a(i - 1)

        @pl.when(i < NC)
        def _():
            got(i, 2)
            got(i, 3)
            pass_copy(i, 10).start()
            pass_copy(i, 11).start()

        @pl.when(i > 0)
        def _():
            add_projection(0, i - 1, quh[...], qdh[...])

        @pl.when(i > 1)
        def _():
            out_sum(i - 2)

        @pl.when(i < NC)
        def _():
            got(i, 4)
            got(i, 5)
            pass_copy(i, 12).start()
            pass_copy(i, 13).start()

        @pl.when(jnp.logical_and(i > 0, i < NC))
        def _():
            work_b(i - 1)

        @pl.when(i < NC)
        def _():
            for slot in range(6, 14):
                got(i, slot)

        return carry

    lax.fori_loop(0, NC + 1, step, 0)

    def mate_copy(ph):
        return send(proj.at[ph, 1 - c], pbuf.at[ph], ars.at[ph, 0], arr.at[ph, 0], dp, mate)

    def rs_copy(ph, t):
        return send(rsb.at[ph, dp_at(t)], rcv.at[ph, dp], ars.at[ph, t], arr.at[ph, t], dp_at(t), mp)

    def y_copy(ph, t):
        to = ((y + t) % N_Y) * 2 + c
        return send(ysend.at[ph], ybuf.at[ph, y], ars.at[ph, 15 + t], arr.at[ph, 15 + t], dp, to)

    def ag_copy(ph, t):
        return send(agb.at[ph, dp], agb.at[ph, dp], ars.at[ph, 18 + t], arr.at[ph, 18 + t], dp_at(t), mp)

    def big_copy(ph):
        return send(bigf.at[ph, c], bigf.at[ph, c], ars.at[ph, 34], arr.at[ph, 34], dp, mate)

    def reduce_start(ph):
        mate_copy(ph).start()

    def reduce_scatter(ph):
        mate_copy(ph).wait_recv()
        own = proj[ph, c] + pbuf[ph]
        sm = small[ph]
        for j in range(N_DP):
            rsb[ph, j, 0:4] = own[4 * j : 4 * j + 4]
            rsb[ph, j, 4:8] = sm[4 * j : 4 * j + 4]
        for t in range(1, N_DP):
            rs_copy(ph, t).start()
        rcv[ph, dp] = rsb[ph, dp]

    def reduce_y(ph):
        for t in range(1, N_DP):
            rs_copy(ph, t).wait_recv()
        total = rcv[ph, 0]
        for j in range(1, N_DP):
            total = total + rcv[ph, j]
        ysend[ph] = total
        for t in range(1, N_Y):
            y_copy(ph, t).start()
        ybuf[ph, y] = total

    def gather_start(ph):
        for t in range(1, N_Y):
            y_copy(ph, t).wait_recv()
        total = ybuf[ph, 0]
        for j in range(1, N_Y):
            total = total + ybuf[ph, j]
        agb[ph, dp, 0:4] = total[0:4]
        agb[ph, dp, 4:8] = ysend[ph, 4:8]
        for t in range(1, N_DP):
            ag_copy(ph, t).start()

    def gather_mate(ph):
        for t in range(1, N_DP):
            ag_copy(ph, t).wait_recv()
        for j in range(N_DP):
            bigf[ph, c, 4 * j : 4 * j + 4] = agb[ph, j, 0:4]
            small[ph, 4 * j : 4 * j + 4] = agb[ph, j, 4:8]
        big_copy(ph).start()

    def gather_end(ph):
        big_copy(ph).wait_recv()
        return jnp.concatenate([bigf[ph, 0], bigf[ph, 1]], axis=1), small[ph]

    def piece(first, owner):
        at = pl.multiple_of((owner // 2) * feats, 32)
        return osb.at[pl.ds(first, HALF), pl.ds(at, feats), :]

    def y_first(k):
        src, dst, to = (
            (piece(0, far), ra, left), (piece(HALF, far), rb, right),
            (piece(0, right), da, right), (piece(HALF, left), db, left),
        )[k]
        return send(src, dst, ys.at[k], yr.at[k], dp, to)

    def y_second(k):
        src, dst, to = ((fa, ea, left), (fb, eb, right))[k]
        return send(src, dst, ys.at[4 + k], yr.at[4 + k], dp, to)

    def own_rows(i, owner):
        return osb[i, pl.ds(pl.multiple_of((owner // 2) * feats, 32), feats), :]

    def out_copy_dp(t, k):
        to = dp_at(t)
        return send(a2s.at[to, k], a2r.at[dp, k], a2ss.at[k, t], a2rr.at[k, t], to, mp)

    def gram_copy(t):
        return send(gbuf.at[mp], gbuf.at[mp], gms.at[t], gmr.at[t], dp, mp_at(t))

    reduce_start(0)
    work_b(NC - 1)
    reduce_scatter(0)
    out_sum(NC - 1)
    for k in range(4):
        y_first(k).start()
    reduce_y(0)
    for k in range(2):
        y_first(k).wait_recv()
    for i in range(HALF):
        fa[i] = (own_rows(i, left).astype(F32) + ra[i].astype(F32)).astype(BF16)
        fb[i] = (own_rows(HALF + i, right).astype(F32) + rb[i].astype(F32)).astype(BF16)
    gather_start(0)
    for k in range(2):
        y_second(k).start()
    gather_mate(0)
    proj_up, proj_down = gather_end(0)
    gram_d = gram_of(proj_down)
    gbuf[mp] = jnp.concatenate([gram_d, jnp.zeros_like(gram_d)], axis=1)
    for t in range(1, N_MP):
        gram_copy(t).start()
    quh[:, :half] = stack2(proj_down)
    qdh[...] = stack2(proj_up)

    def fresh(i, carry):
        add_projection(1, i, qdh[...], quh[...])
        return carry

    lax.fori_loop(0, NC, fresh, 0)
    reduce_start(1)
    for k in range(2, 4):
        y_first(k).wait_recv()
    for k in range(2):
        y_second(k).wait_recv()
    reduce_scatter(1)
    per = tc // BLOCK
    for i in range(NC):
        direct, summed = (da, ea) if i < HALF else (db, eb)
        j = i % HALF
        total = own_rows(i, mp).astype(F32) + direct[j].astype(F32) + summed[j].astype(F32)
        total = jnp.where(keep[i] > 0, total, 0.0).astype(BF16)
        for b in range(per):
            ob[i * per + b] = total[:, b * BLOCK : (b + 1) * BLOCK]
    for j in range(N_DP):
        for k in range(CAP):
            a2s[j, k] = ob[slot_idx[j * CAP + k]]
    for k in range(CAP):
        for t in range(1, N_DP):
            out_copy_dp(t, k).start()
    a2r[dp] = a2s[dp]
    for t in range(1, N_MP):
        gram_copy(t).wait_recv()
    total_gram = gbuf[0]
    for j in range(1, N_MP):
        total_gram = total_gram + gbuf[j]
    grams = jnp.stack([gram_of(proj_up), total_gram[:, :RANK]])
    inv = inverse_factors(grams)
    inv_u, inv_d = left3(inv[0].T), left3(inv[1].T)
    a3u[...] = left3(mm_tn(inv_u, right3(proj_up)))
    a3d[...] = left3(mm_tn(inv_d, right3(proj_down)))
    reduce_y(1)
    gather_start(1)
    gather_mate(1)
    fresh_down, fresh_up = gather_end(1)
    new_u = mm_tn(inv_u, right3(fresh_up))
    new_d = mm_tn(inv_d, right3(fresh_down))
    qnu[...] = new_u
    qnd[...] = new_d
    b3u[...] = right3(new_u)
    b3d[...] = right3(new_d)
    for k in range(CAP):
        for t in range(1, N_DP):
            out_copy_dp(t, k).wait_recv()
    for t in range(1, N_DP):
        send(er, erb.at[dp], ers.at[t], err_.at[t], dp_at(t), mp).wait()
    era_out[...] = erb[...]
    for j in range(N_DP):
        for k in range(CAP):
            a2o[j * CAP + k] = a2r[j, k]

    def sent(i, carry):
        for slot in range(14):
            (own_copy if slot in (0, 1, 2, 3, 6, 7) else pass_copy)(i, slot).wait_send()
        out_copy(i).wait_send()
        return carry

    lax.fori_loop(0, NC, sent, 0)
    for ph in range(2):
        mate_copy(ph).wait_send()
        big_copy(ph).wait_send()
        for t in range(1, N_Y):
            y_copy(ph, t).wait_send()
        for t in range(1, N_DP):
            rs_copy(ph, t).wait_send()
            ag_copy(ph, t).wait_send()
    for k in range(4):
        y_first(k).wait_send()
    for k in range(2):
        y_second(k).wait_send()
    for k in range(CAP):
        for t in range(1, N_DP):
            out_copy_dp(t, k).wait_send()
    for t in range(1, N_MP):
        gram_copy(t).wait_send()


def layer_kernel(slot_idx, xin, cin, wu, wd, qu, qd, er, keep):
    _, feats, tc = xin.shape
    width, ff = wu.shape
    half = width // 2
    vm = pl.BlockSpec(memory_space=pltpu.VMEM)
    shape = jax.ShapeDtypeStruct
    outs = [
        shape((N_DP * CAP, feats, BLOCK), BF16),
        shape((N_DP, 8, 128), jnp.int32),
        shape((3 * RANK, width), BF16),
        shape((3 * RANK, ff), BF16),
        shape((3 * RANK, ff), BF16),
        shape((3 * RANK, width), BF16),
        shape((RANK, ff), F32),
        shape((RANK, width), F32),
    ]
    dma = pltpu.SemaphoreType.DMA
    scratch = [
        pltpu.VMEM((NC, width, tc), BF16),
        pltpu.VMEM((NC, width, tc), BF16),
        pltpu.VMEM((NC, ff, tc), BF16),
        pltpu.VMEM((NC, ff, tc), BF16),
        pltpu.VMEM((ff, width), BF16),
        pltpu.VMEM((width, ff), BF16),
        pltpu.VMEM((2 * RANK, ff), BF16),
        pltpu.VMEM((2 * RANK, width), BF16),
        pltpu.VMEM((2, 2, RANK, half), F32),
        pltpu.VMEM((2, RANK, ff), F32),
        pltpu.VMEM((2, RANK, half), F32),
        pltpu.VMEM((2, N_DP, 8, half), F32),
        pltpu.VMEM((2, N_DP, 8, half), F32),
        pltpu.VMEM((2, 8, half), F32),
        pltpu.VMEM((2, N_Y, 8, half), F32),
        pltpu.VMEM((2, N_DP, 8, half), F32),
        pltpu.VMEM((2, 2, RANK, half), F32),
        pltpu.VMEM((N_MP, RANK, 128), F32),
        pltpu.VMEM((NC, 2, N_Y * feats, tc), BF16),
        pltpu.VMEM((NC, N_Y * feats, tc), BF16),
        pltpu.VMEM((NC, N_Y * feats, tc), BF16),
    ]
    scratch += [pltpu.VMEM((HALF, feats, tc), BF16) for _ in range(8)]
    scratch += [
        pltpu.VMEM((NC * tc // BLOCK, feats, BLOCK), BF16),
        pltpu.VMEM((N_DP, CAP, feats, BLOCK), BF16),
        pltpu.VMEM((N_DP, CAP, feats, BLOCK), BF16),
        pltpu.VMEM((N_DP, 8, 128), jnp.int32),
        dma((NC, 14)),
        dma((NC, 14)),
        dma((NC,)),
        dma((NC,)),
        dma((6,)),
        dma((6,)),
        dma((2, 35)),
        dma((2, 35)),
        dma((N_MP,)),
        dma((N_MP,)),
        dma((N_DP,)),
        dma((N_DP,)),
        dma((CAP, N_DP)),
        dma((CAP, N_DP)),
    ]
    return pl.pallas_call(
        kernel_body,
        out_shape=outs,
        in_specs=[pl.BlockSpec(memory_space=pltpu.SMEM)] + [vm] * 8,
        out_specs=[vm] * len(outs),
        scratch_shapes=scratch,
        compiler_params=pltpu.CompilerParams(
            collective_id=0, has_side_effects=True, vmem_limit_bytes=60 * 1024 * 1024
        ),
        name="layer",
    )(slot_idx, xin, cin, wu, wd, qu, qd, er, keep)


def place_body(ranks, blocks, out):
    me = lax.axis_index("dp")
    per = ranks.shape[1]

    out[...] = jnp.zeros_like(out)

    def source(r, filled):
        seen = jnp.int32(0)
        for b in range(per):
            mine = ranks[r, b] == me

            @pl.when(mine)
            def _(seen=seen, filled=filled):
                out[filled] = blocks[r * CAP + seen]

            step = mine.astype(jnp.int32)
            seen = seen + step
            filled = filled + step
        return filled

    lax.fori_loop(0, N_DP, source, jnp.int32(0))


def place(ranks, blocks):
    return pl.pallas_call(
        place_body,
        out_shape=jax.ShapeDtypeStruct((RMAX, *blocks.shape[1:]), blocks.dtype),
        in_specs=[
            pl.BlockSpec(memory_space=pltpu.SMEM),
            pl.BlockSpec(memory_space=pltpu.VMEM),
        ],
        out_specs=pl.BlockSpec(memory_space=pltpu.VMEM),
        name="place",
    )(ranks, blocks)


def send_slots(ranks):
    count = ranks.shape[0]
    ids = jnp.arange(count, dtype=jnp.int32)
    before = (ranks[None, :] == ranks[:, None]) & (ids[None, :] < ids[:, None])
    target = ranks * CAP + jnp.sum(before.astype(jnp.int32), axis=1)
    places = jnp.arange(N_DP * CAP, dtype=jnp.int32)
    return jnp.sum(jnp.where(places[:, None] == target[None, :], ids[None, :], 0), axis=1).astype(jnp.int32)


def chunked(rows):
    tokens, feats = rows.shape
    return rows.reshape(NC, tokens // NC, feats).transpose(0, 2, 1)


def local(patches, cotangent, encoder_rank, block_fill, w_up, w_down, q_up, q_down):
    tokens, feats = patches.shape
    blocks = encoder_rank.shape[0]
    within = jnp.arange(BLOCK, dtype=jnp.int32)
    kept = within[None, :] < block_fill[:, None]
    masked = jnp.where(kept.reshape(-1, 1), cotangent, jnp.zeros((), BF16))
    keep = kept.astype(F32).reshape(NC, 1, tokens // NC)
    er = jnp.broadcast_to(jnp.pad(encoder_rank, (0, 128 - blocks))[None, :], (8, 128))
    landed, ranks, a3u, b3u, a3d, b3d, qnu, qnd = layer_kernel(
        send_slots(encoder_rank), chunked(patches), chunked(masked), w_up, w_down,
        q_up.T, q_down.T, er, keep,
    )
    placed = place(ranks[:, 0, :blocks], landed)
    encoded = placed.transpose(0, 2, 1).reshape(RMAX * BLOCK, feats)
    approx_up = mm_tn(a3u, b3u)
    approx_down = mm_tn(a3d, b3d)
    return (encoded, approx_up, approx_down, qnu.T, qnd.T)


def solution(mesh):
    in_specs = (
        P("dp", "mp"), P("dp", "mp"), P("dp"), P("dp"), P(None, "mp"), P("mp", None), P("mp", None), P(),
    )
    out_specs = (P("dp", "mp"), P(None, "mp"), P("mp", None), P("mp", None), P())
    return jax.shard_map(local, mesh=mesh, in_specs=in_specs, out_specs=out_specs, check_vma=False)
```

time: 401 us -> 139 us (0.35)
  waiting for transfers between devices: 187 us -> 0 us
  Pallas kernels: 0 us -> 119 us
  blocking collectives: 53.4 us -> 0 us
  matrix products: 46.6 us -> 4.79 us
  other arithmetic: 35.9 us -> 4.57 us
  starting transfers between devices: 28.3 us -> 0 us
  local copies, waits for them, and re-layouts: 33.2 us -> 9.08 us
  between operations: 15.1 us -> 0.68 us
    pallas_call x0 -> x2, Pallas kernels: none -> 119 us  [the longest x1 115 us: layer_kernel(): pl.pallas_call(kernel_body, out_shape=outs, in_specs=[pl.BlockSpec(memory...]
    psum x4 -> x0, waiting for transfers between devices: 104 us -> none  [over_axes(): shard = lax.psum(shard, axis)]
    all_gather x1 -> x0, waiting for transfers between devices: 51.1 us -> none  [rows_first(): whole, at, done = (lax.all_gather(both, axis, axis=0, tiled=True), 0, [])]
    dot_general x14 -> x2, matrix products: 44.2 us -> 4.79 us  [mm_tn(): return lax.dot_general(a, b, TN, preferred_element_type=F32)]
    all_gather x4 -> x0, blocking collectives: 33.4 us -> none  [all_blocks(): blocks = lax.all_gather(blocks, axes[k], axis=0, tiled=True)]
    all_to_all x5 -> x0, waiting for transfers between devices: 30.9 us -> none  [the longest x3 30.9 us: copy_for_each(): lax.all_to_all(jnp.broadcast_to(shard[None], (count, *shard.shape)), axis...]
    all_to_all x5 -> x0, starting transfers between devices: 27.4 us -> none  [the longest x3 17.8 us: copy_for_each(): lax.all_to_all(jnp.broadcast_to(shard[None], (count, *shard.shape)), axis...]
    another operation x11 -> x0, other arithmetic: 24.8 us -> none  [the longest x6 13 us: orthonormal(): lower = jnp.linalg.cholesky(gram)]
  transfers between devices with their start and end apart: 13 -> 0, of which waited for: 7 -> 0; matrix products, arithmetic and copies ran while one was open for 23% -> 0% of each run, Pallas kernels for 0% -> 0%
where the time goes in v1:
time: 139 us
  Pallas kernels  119 us (86%)
  local copies, waits for them, and re-layouts  9.08 us (7%)
  matrix products  4.79 us (3%)
  other arithmetic  4.57 us (3%)
    pallas_call x1, Pallas kernels, layer_kernel(): pl.pallas_call(kernel_body, out_shape=outs, in_specs=[pl.BlockSpec(memory...  115 us
    dot_general x2, matrix products, mm_tn(): return lax.dot_general(a, b, TN, preferred_element_type=F32)  4.79 us
    pallas_call x1, Pallas kernels, place(): pl.pallas_call(place_body, out_shape=jax.ShapeDtypeStruct((RMAX, *blocks....  4.36 us

profile of v1, /device:TPU:1, one launch (start us, length us, event | category | flops | bytes accessed | tf_op | source)
XLA Modules:
  0.0 138.6 jit_solution(8459314413137564128)
XLA Ops:
  0.6 0.7 pad.4
  1.3 0.9 convert_reduce_fusion
  2.2 0.7 multiply_add_fusion
  2.9 0.6 select_reduce_fusion.slot_idx
  3.5 0.7 fusion.1
  4.2 0.6 broadcast_in_dim.43.er
  4.8 0.7 lt.64
  5.5 0.1 lt.65
  5.6 0.6 compare_convert_fusion.keep
  6.2 1.1 broadcast_select_fusion
  7.3 2.1 %bitcast_bitcast_fusion = (bf16[6,160,256]{2,1,0:T(8,128)(2,1)}, bf16[6,160,256]{2,1,0:T(8,128)(2,1)}) fusion(bf16[20,6,8,256]{3,2,1,0:T(8,128)(2,1)S(1)} %bitcast.31, bf16[20,6,8,256]{3,2,1,0:T(8,128)(2,1)} %bitcast.32), kind=kLoop, calls=%fused_computation.1 | loop fusion | bytes 1966080 | tf_op jit(solution)/shard_map/transpose | solution.py:578
  9.3 115.1 %layer.1 = (bf16[32,160,128]{2,1,0:T(8,128)(2,1)}, s32[16,8,128]{2,1,0:T(8,128)}, bf16[192,1280]{1,0:T(8,128)(2,1)}, bf16[192,640]{1,0:T(8,128)(2,1)}, bf16[192,...) custom-call(s32[32]{0:T(128)} %select_reduce_fusion.slot_idx, ...), custom_call_target="tpu_custom_call" | custom-call | tf_op jit(solution)/shard_map/layer/pallas_call | solution.py:518
  124.5 0.0 copy-start.1
  124.5 0.0 copy-start.4
  124.5 0.9 copy.20
  125.4 0.6 slice_bitcast_fusion.ranks
  126.0 4.4 %place.1 = bf16[18,160,128]{2,1,0:T(8,128)(2,1)} custom-call(s32[16,12]{1,0:T(8,128)} %slice_bitcast_fusion.ranks, bf16[32,160,128]{2,1,0:T(8,128)(2,1)} %get-tuple-element.14.blocks), custom_call_target="tpu_custom_call" | custom-call | tf_op jit(solution)/shard_map/place/pallas_call | solution.py:555
  130.4 2.0 %copy_bitcast_fusion = bf16[2304,160]{0,1:T(8,128)(2,1)} fusion(bf16[18,160,128]{2,1,0:T(8,128)(2,1)} %place.1), kind=kLoop, calls=%fused_computation | loop fusion | bytes 1474560 | tf_op jit(solution)/shard_map/reshape | solution.py:594
  132.4 0.0 copy-done.4
  132.4 2.4 %fusion.2 = f32[1280,640]{1,0:T(8,128)} fusion(bf16[192,1280]{1,0:T(8,128)(2,1)S(1)} %copy-done.1, bf16[192,640]{1,0:T(8,128)(2,1)S(1)} %copy-done.4), kind=kOutput, calls=%fused_computation.15 | convolution fusion | flops 314572800 | bytes 4014080 | tf_op jit(solution)/shard_map/dot_general | solution.py:34
  134.8 0.0 copy-done.3
  134.8 2.4 %fusion.3 = f32[640,1280]{1,0:T(8,128)} fusion(bf16[192,640]{1,0:T(8,128)(2,1)S(1)} %copy-done.3, bf16[192,1280]{1,0:T(8,128)(2,1)S(1)} %copy-done), kind=kOutput, calls=%fused_computation.16 | convolution fusion | flops 314572800 | bytes 4014080 | tf_op jit(solution)/shard_map/dot_general | solution.py:34
  137.2 0.7 copy.30
  137.9 0.7 copy.31
  (9 shorter events, 0.0 us)
Async XLA Ops:
  124.5 7.9 %copy-start.1 = (bf16[192,1280]{1,0:T(8,128)(2,1)S(1)}, bf16[192,1280]{1,0:T(8,128)(2,1)}, u32[]{:S(2)}) copy-start(bf16[192,1280]{1,0:T(8,128)(2,1)} %get-tuple-element.15) | copy-start | bytes 1474564
  124.5 7.9 %copy-start.4 = (bf16[192,640]{1,0:T(8,128)(2,1)S(1)}, bf16[192,640]{1,0:T(8,128)(2,1)}, u32[]{:S(2)}) copy-start(bf16[192,640]{1,0:T(8,128)(2,1)} %get-tuple-element.16) | copy-start | bytes 737284
  126.0 8.8 %copy-start = (bf16[192,1280]{1,0:T(8,128)(2,1)S(1)}, bf16[192,1280]{1,0:T(8,128)(2,1)}, u32[]{:S(2)}) copy-start(bf16[192,1280]{1,0:T(8,128)(2,1)} %get-tuple-element.18) | copy-start | bytes 1474564
  126.0 8.8 %copy-start.3 = (bf16[192,640]{1,0:T(8,128)(2,1)S(1)}, bf16[192,640]{1,0:T(8,128)(2,1)}, u32[]{:S(2)}) copy-start(bf16[192,640]{1,0:T(8,128)(2,1)} %get-tuple-element.17) | copy-start | bytes 737284
  132.4 4.8 %copy-start.5 = (f32[64,640]{1,0:T(8,128)S(1)}, f32[64,640]{1,0:T(8,128)}, u32[]{:S(2)}) copy-start(f32[64,640]{1,0:T(8,128)} %get-tuple-element.19) | copy-start | bytes 491524
  132.4 5.5 %copy-start.2 = (f32[64,1280]{1,0:T(8,128)S(1)}, f32[64,1280]{1,0:T(8,128)}, u32[]{:S(2)}) copy-start(f32[64,1280]{1,0:T(8,128)} %get-tuple-element.20) | copy-start | bytes 983044

commit v2 on v0

v2 whole, which is shorter than its diff:
```python
import jax
import jax.numpy as jnp
from jax import lax
from jax.experimental import pallas as pl
from jax.experimental.pallas import tpu as pltpu
from jax.sharding import PartitionSpec as P

BLOCK = 128
CAP = 2
RMAX = 18
BLK_DEV = 12
N_DP = 16
N_Y = 4
N_MP = 8
RANK = 64
NC = 6
HALF = NC // 2
AHEAD = 2
MESH = pl.DeviceIdType.MESH
F32 = jnp.float32
BF16 = jnp.bfloat16
NT = (((1,), (1,)), ((), ()))
TN = (((0,), (0,)), ((), ()))


def mm(a, b):
    return jnp.dot(a, b, preferred_element_type=F32)


def mm_nt(a, b):
    return lax.dot_general(a, b, NT, preferred_element_type=F32)


def mm_tn(a, b):
    return lax.dot_general(a, b, TN, preferred_element_type=F32)


def parts(v):
    hi = v.astype(BF16)
    lo = (v - hi.astype(F32)).astype(BF16)
    return hi, lo


def stack2(v):
    return jnp.concatenate(parts(v), axis=0)


def fold2(v):
    return v[:RANK] + v[RANK:]


def left4(v):
    hi, lo = parts(v)
    return jnp.concatenate([hi, hi, lo, lo], axis=0)


def right4(v):
    hi, lo = parts(v)
    return jnp.concatenate([hi, lo, hi, lo], axis=0)


def gram_of(v):
    s = stack2(v)
    g = mm_nt(s, s)
    return g[:RANK, :RANK] + g[:RANK, RANK:] + g[RANK:, :RANK] + g[RANK:, RANK:]


def eliminate(w, first, last):
    row = lax.broadcasted_iota(jnp.int32, w.shape, 1)
    for k in range(first, last):
        pivot = w[:, k : k + 1, k : k + 1]
        line = w[:, k : k + 1, :] * (1.0 / pivot)
        w = w - jnp.where(row > k, w[:, :, k : k + 1] * line, 0.0)
    return w


def identity_at_right(shape):
    row = lax.broadcasted_iota(jnp.int32, shape, 0)
    lane = lax.broadcasted_iota(jnp.int32, shape, 1)
    return jnp.where(lane == row + RANK, 1.0, 0.0).astype(F32)


def inverse_of_factor(w):
    row = lax.broadcasted_iota(jnp.int32, w.shape, 0)
    lane = lax.broadcasted_iota(jnp.int32, w.shape, 1)
    diag = jnp.sum(jnp.where(lane == row, w, 0.0), axis=1, keepdims=True)
    return (w * lax.rsqrt(diag))[:, RANK:]


def kernel_body(
    ranks, fills, pt, ct, wu, wd, qu, qd,
    a2o, a4u, a4d, era_out, qnu, qnd,
    xall, call, hid, gp, wus, wds, qus, qds, wut, wdt, quh, qdh,
    proj, small, pbuf, rsb, rcv, ysend, ybuf, agb, bigf, elim,
    gbuf, outp, po, osb, ra, rb, da, db, fa, fb, ea, eb, ob, a2s, f4u, f4d, ers, erb,
    lsem, nsem, msem, gsem, osem, ossem, ysem, yssem, arr, ars, mrr, mrs, xr, xs, a2rr, a2ss,
):
    dp = lax.axis_index("dp")
    mp = lax.axis_index("mp")
    y = mp // 2
    c = mp % 2
    right = ((y + 1) % N_Y) * 2 + c
    left = ((y + 3) % N_Y) * 2 + c
    far = ((y + 2) % N_Y) * 2 + c
    mate = y * 2 + (1 - c)
    feats = pt.shape[0]
    tc = xall.shape[2]
    per = tc // BLOCK
    blocks = NC * per
    half = proj.shape[3]

    def send(src, dst, ssem, rsem, dpi, mpi):
        return pltpu.make_async_remote_copy(
            src_ref=src, dst_ref=dst, send_sem=ssem, recv_sem=rsem,
            device_id=(dpi, mpi), device_id_type=MESH,
        )

    def arrived(ref, sem):
        send(ref, ref, sem, sem, dp, mate).wait_recv()

    def left_here(ref, sem):
        send(ref, ref, sem, sem, dp, mate).wait_send()

    def fetched(ref, sem):
        pltpu.make_async_copy(ref, ref, sem).wait()

    def dp_at(t):
        return (dp + t) % N_DP

    def mp_at(t):
        return (mp + t) % N_MP

    def rows(ref, i, owner):
        return ref.at[i, pl.ds(pl.multiple_of(owner * feats, 32), feats), :]

    barrier = pltpu.get_barrier_semaphore()
    for t in range(1, N_DP):
        pl.semaphore_signal(barrier, inc=1, device_id=(dp_at(t), mp), device_id_type=MESH)
    for t in range(1, N_MP):
        pl.semaphore_signal(barrier, inc=1, device_id=(dp, mp_at(t)), device_id_type=MESH)

    for i in range(NC):
        pltpu.make_async_copy(ct.at[:, pl.ds(i * tc, tc)], rows(call, i, mp), lsem.at[0]).start()
    for i in range(NC):
        pltpu.make_async_copy(pt.at[:, pl.ds(i * tc, tc)], rows(xall, i, mp), lsem.at[1]).start()
    weights = ((wu, wus), (wd, wds), (qu, qus), (qd, qds))
    for k, (src, dst) in enumerate(weights):
        pltpu.make_async_copy(src, dst, lsem.at[2 + k]).start()
    lane8 = lax.broadcasted_iota(jnp.int32, (8, 128), 1)
    mine = jnp.zeros((8, 128), jnp.int32)
    for b in range(blocks):
        mine = jnp.where(lane8 == b, ranks[b], mine)
    ers[...] = mine
    erb[dp] = mine
    token = lax.broadcasted_iota(jnp.int32, (feats, BLOCK), 1)
    def mask_cot(i):
        place_at = pl.ds(pl.multiple_of(mp * feats, 32), feats)
        for k in range(per):
            lanes = slice(k * BLOCK, (k + 1) * BLOCK)
            kept = jnp.where(token < fills[i * per + k], call[i, place_at, lanes].astype(F32), 0.0)
            call[i, place_at, lanes] = kept.astype(BF16)

    fetched(call.at[0, pl.ds(0, NC * feats), :], lsem.at[0])
    for i in range(AHEAD):
        mask_cot(i)
    fetched(xall.at[0, pl.ds(0, NC * feats), :], lsem.at[1])
    pl.semaphore_wait(barrier, N_DP + N_MP - 2)

    def pass_on(ref, which, i, owner, to, rsem):
        send(rows(ref, i, owner), rows(ref, i, owner), gsem.at[which], rsem, dp, to).start()

    def start_own(i):
        pass_on(xall, 0, i, mp, right, nsem.at[i, 0])
        pass_on(call, 1, i, mp, left, nsem.at[i, 0])
        pass_on(call, 1, i, mp, right, nsem.at[i, 1])
        pass_on(xall, 0, i, mp, left, nsem.at[i, 1])

    def pair(i):
        return xall.at[i, pl.ds(0, 2 * feats), :]

    for i in range(AHEAD):
        start_own(i)
    for i in range(AHEAD, NC):
        mask_cot(i)
    for i in range(NC):
        pass_on(xall, 0, i, mp, mate, msem.at[i])
        pass_on(call, 1, i, mp, mate, msem.at[i])
    for t in range(1, N_DP):
        send(ers, erb.at[dp], xs.at[0], xr.at[0], dp_at(t), mp).start()

    for k, (src, dst) in enumerate(weights):
        fetched(dst, lsem.at[2 + k])
    for j in range(wus.shape[1] // 128):
        wut[j * 128 : (j + 1) * 128, :] = wus[:, j * 128 : (j + 1) * 128].T
    for j in range(wds.shape[1] // 128):
        wdt[j * 128 : (j + 1) * 128, :] = wds[:, j * 128 : (j + 1) * 128].T
    quh[...] = stack2(qus[...])
    qdh[...] = stack2(qds[...])
    for ph in range(2):
        proj[ph] = jnp.zeros_like(proj[ph])
        small[ph] = jnp.zeros_like(small[ph])

    def start_out(i):
        send(outp.at[i, 1 - c], po.at[i], ossem.at[0], osem.at[i], dp, mate).start()

    def out_sum(i):
        arrived(po.at[i], osem.at[i])
        osb[i] = (outp[i, c].astype(F32) + po[i].astype(F32)).astype(BF16)

    def work_a(i):
        pre = mm(wut[...], xall[i])
        grad = mm(wds[...], call[i])
        sig = jax.nn.sigmoid(1.702 * pre)
        act = pre * sig
        hid[i] = act.astype(BF16)
        gp[i] = (grad * (sig + 1.702 * act * (1.0 - sig))).astype(BF16)

    def work_b(i):
        o = mm(wdt[...], hid[i]).astype(BF16)
        for m in range(N_MP):
            at = (m // 2) * feats
            outp[i, m % 2, at : at + feats, :] = o[m * feats : (m + 1) * feats]
        start_out(i)

    def big_add(ph, rows64, other):
        big = fold2(mm_nt(stack2(rows64), other))
        proj[ph, 0] += big[:, :half]
        proj[ph, 1] += big[:, half:]

    def small_add(ph, rows64, other):
        small[ph] += fold2(mm_nt(stack2(rows64), other))

    def add_projection(i):
        big_add(0, fold2(mm(quh[...], gp[i])), xall[i])
        small_add(0, fold2(mm(qdh[...], call[i])), hid[i])

    def piece(first, owner):
        at = pl.multiple_of((owner // 2) * feats, 32)
        return osb.at[pl.ds(first, HALF), pl.ds(at, feats), :]

    def own_rows(i, owner):
        return osb[i, pl.ds(pl.multiple_of((owner // 2) * feats, 32), feats), :]

    def send_b(i):
        j = i - HALF
        y_send(osb.at[i, pl.ds(pl.multiple_of((far // 2) * feats, 32), feats), :], rb.at[j], 1, right)
        y_send(osb.at[i, pl.ds(pl.multiple_of((left // 2) * feats, 32), feats), :], db.at[j], 5, left)

    def y_send(src, dst, group, to):
        send(src, dst, yssem.at[group], ysem.at[group], dp, to).start()

    def step(i, carry):
        @pl.when(i < NC)
        def _():
            arrived(pair(i), nsem.at[i, 0])
            pass_on(xall, 0, i, left, right, nsem.at[i, 2])
            pass_on(call, 1, i, right, left, nsem.at[i, 2])

            @pl.when(i + AHEAD < NC)
            def _():
                start_own(i + AHEAD)

            pass_on(xall, 0, i, left, mate, msem.at[i])
            pass_on(call, 1, i, right, mate, msem.at[i])

        @pl.when(i > 1)
        def _():
            arrived(xall.at[i - 2], msem.at[i - 2])
            work_a(i - 2)

        @pl.when(i < NC)
        def _():
            arrived(pair(i), nsem.at[i, 1])
            pass_on(call, 1, i, left, mate, msem.at[i])
            pass_on(xall, 0, i, right, mate, msem.at[i])

        @pl.when(i > 1)
        def _():
            add_projection(i - 2)

        @pl.when(jnp.logical_and(i > 2, i <= NC))
        def _():
            out_sum(i - 3)

        @pl.when(i == NC)
        def _():
            y_send(piece(0, far), ra, 0, left)
            y_send(piece(0, right), da, 4, right)
            send_b(HALF)

        @pl.when(jnp.logical_and(i > 0, i <= NC))
        def _():
            arrived(pair(i - 1), nsem.at[i - 1, 2])
            pass_on(xall, 0, i - 1, far, mate, msem.at[i - 1])
            pass_on(call, 1, i - 1, far, mate, msem.at[i - 1])

        @pl.when(jnp.logical_and(i > 1, i < NC))
        def _():
            work_b(i - 2)

        return carry

    lax.fori_loop(0, NC + 2, step, 0)

    def mate_start(ph):
        send(proj.at[ph, 1 - c], pbuf.at[ph], mrs.at[ph, 0], mrr.at[ph, 0], dp, mate).start()

    def mate_end(ph):
        arrived(pbuf.at[ph], mrr.at[ph, 0])
        return proj[ph, c] + pbuf[ph]

    def scatter(q, value):
        for j in range(N_DP):
            rsb[q, j] = value[4 * j : 4 * j + 4]
        for t in range(1, N_DP):
            to = dp_at(t)
            send(rsb.at[q, to], rcv.at[q, dp], ars.at[q, 0], arr.at[q, 0], to, mp).start()
        rcv[q, dp] = rsb[q, dp]

    def collect(q):
        arrived(rcv.at[q, pl.ds(0, N_DP - 1)], arr.at[q, 0])
        total = rcv[q, 0]
        for j in range(1, N_DP):
            total = total + rcv[q, j]
        return total

    def y_start(ph, q, total):
        ysend[ph] = total
        for t in range(1, N_Y):
            to = ((y + t) % N_Y) * 2 + c
            send(ysend.at[ph], ybuf.at[ph, y], ars.at[q, 2], arr.at[q, 2], dp, to).start()
        ybuf[ph, y] = total

    def y_end(ph, q):
        arrived(ybuf.at[ph, pl.ds(0, N_Y - 1)], arr.at[q, 2])
        total = ybuf[ph, 0]
        for j in range(1, N_Y):
            total = total + ybuf[ph, j]
        return total

    def spread(q, total):
        agb[q, dp] = total
        for t in range(1, N_DP):
            send(agb.at[q, dp], agb.at[q, dp], ars.at[q, 1], arr.at[q, 1], dp_at(t), mp).start()

    def small_end(ph, q):
        arrived(agb.at[q, pl.ds(0, N_DP - 1)], arr.at[q, 1])
        for j in range(N_DP):
            small[ph, 4 * j : 4 * j + 4] = agb[q, j]
        return small[ph]

    def big_start(ph, q):
        arrived(agb.at[q, pl.ds(0, N_DP - 1)], arr.at[q, 1])
        for j in range(N_DP):
            bigf[ph, c, 4 * j : 4 * j + 4] = agb[q, j]
        send(bigf.at[ph, c], bigf.at[ph, c], mrs.at[ph, 1], mrr.at[ph, 1], dp, mate).start()

    def big_end(ph):
        arrived(bigf.at[ph, 0], mrr.at[ph, 1])
        return jnp.concatenate([bigf[ph, 0], bigf[ph, 1]], axis=1)

    def start_slots(k, first, last):
        for t in range(first, last):
            to = dp_at(t)
            send(a2s.at[k, to], a2o.at[k, dp], a2ss.at[k], a2rr.at[k], to, mp).start()

    def out_landed(k):
        arrived(a2o.at[k, pl.ds(0, N_DP - 1)], a2rr.at[k])

    mate_start(0)
    scatter(1, small[0])
    work_b(NC - 2)
    scatter(0, mate_end(0))
    work_b(NC - 1)
    for i in range(HALF + 1, NC):
        out_sum(i)
        send_b(i)
    arrived(ra, ysem.at[0])
    for i in range(HALF):
        fa[i] = (own_rows(i, left).astype(F32) + ra[i].astype(F32)).astype(BF16)
    spread(1, collect(1))
    y_start(0, 0, collect(0))
    y_send(fa, ea, 2, left)
    spread(0, y_end(0, 0))
    arrived(rb, ysem.at[1])
    for i in range(HALF):
        fb[i] = (own_rows(HALF + i, right).astype(F32) + rb[i].astype(F32)).astype(BF16)
    y_send(fb, eb, 3, right)
    proj_down = small_end(0, 1)
    quh[:, :half] = stack2(proj_down)

    def fresh_down(i, carry):
        big_add(1, fold2(mm(quh[...], hid[i])), call[i])
        return carry

    lax.fori_loop(0, NC, fresh_down, 0)
    mate_start(1)
    gram_d = gram_of(proj_down)
    gbuf[mp] = jnp.concatenate([gram_d[: RANK // 2], gram_d[RANK // 2 :]], axis=1)
    for t in range(1, N_MP):
        send(gbuf.at[mp], gbuf.at[mp], xs.at[1], xr.at[1], dp, mp_at(t)).start()
    big_start(0, 0)
    scatter(2, mate_end(1))
    proj_up = big_end(0)
    qdh[...] = stack2(proj_up)

    def fresh_up(i, carry):
        small_add(1, fold2(mm(qdh[...], xall[i])), gp[i])
        return carry

    lax.fori_loop(0, HALF, fresh_up, 0)
    arrived(ea, ysem.at[2])
    arrived(eb, ysem.at[3])
    arrived(da, ysem.at[4])
    arrived(db, ysem.at[5])
    for b in range(blocks):
        i, at = b // per, (b % per) * BLOCK
        direct, summed = (da, ea) if i < HALF else (db, eb)
        lanes = slice(at, at + BLOCK)
        total = own_rows(i, mp)[:, lanes].astype(F32)
        total = total + direct[i % HALF, :, lanes].astype(F32) + summed[i % HALF, :, lanes].astype(F32)
        ob[b] = jnp.where(token < fills[b], total, 0.0).astype(BF16)
    for j in range(N_DP):
        first = jnp.int32(0)
        second = jnp.int32(0)
        for b in range(blocks - 1, -1, -1):
            here = ranks[b] == j
            second = jnp.where(here, first, second)
            first = jnp.where(here, b, first)
        a2s[0, j] = ob[first]
        a2s[1, j] = ob[second]
    start_slots(0, 1, 8)
    for k in range(CAP):
        pltpu.make_async_copy(a2s.at[k, dp], a2o.at[k, dp], lsem.at[k]).start()
    lax.fori_loop(HALF, NC, fresh_up, 0)
    scatter(3, small[1])
    start_slots(0, 8, N_DP)
    y_start(1, 2, collect(2))
    elim[0] = identity_at_right((RANK, 2 * RANK))
    elim[0, :, :RANK] = gram_of(proj_up)
    arrived(gbuf.at[pl.ds(0, N_MP - 1)], xr.at[1])
    gram_d = gbuf[0]
    for j in range(1, N_MP):
        gram_d = gram_d + gbuf[j]
    elim[1] = identity_at_right((RANK, 2 * RANK))
    elim[1, : RANK // 2, :RANK] = gram_d[:, :RANK]
    elim[1, RANK // 2 :, :RANK] = gram_d[:, RANK:]
    elim[...] = eliminate(elim[...], 0, 8)
    spread(2, y_end(1, 2))
    start_slots(1, 1, 8)
    elim[...] = eliminate(elim[...], 8, 24)
    spread(3, collect(3))
    start_slots(1, 8, N_DP)
    elim[...] = eliminate(elim[...], 24, RANK - 1)
    inv_u = left4(inverse_of_factor(elim[0]).T)
    inv_d = left4(inverse_of_factor(elim[1]).T)
    f4u[...] = left4(mm_tn(inv_u, right4(proj_up))).T
    f4d[...] = left4(mm_tn(inv_d, right4(proj_down))).T
    pltpu.make_async_copy(f4u, a4u, lsem.at[2]).start()
    pltpu.make_async_copy(f4d, a4d, lsem.at[3]).start()
    arrived(erb.at[pl.ds(0, N_DP - 1)], xr.at[0])
    for r in range(N_DP):
        era_out[r : r + 1, :] = erb[r, 0:1, :]
    big_start(1, 2)
    out_landed(0)
    new_u = mm_tn(inv_u, right4(small_end(1, 3)))
    qnu[...] = new_u
    new_d = mm_tn(inv_d, right4(big_end(1)))
    qnd[...] = new_d
    out_landed(1)

    pltpu.make_async_copy(f4u, a4u, lsem.at[2]).wait()
    pltpu.make_async_copy(f4d, a4d, lsem.at[3]).wait()
    left_here(xall.at[:, pl.ds(0, 7 * feats), :], gsem.at[0])
    left_here(call.at[:, pl.ds(0, 7 * feats), :], gsem.at[1])
    left_here(po, ossem.at[0])
    left_here(erb.at[pl.ds(0, N_DP - 1)], xs.at[0])
    left_here(gbuf.at[pl.ds(0, N_MP - 1)], xs.at[1])
    for group, ref in enumerate((ra, rb, ea, eb, da, db)):
        left_here(ref, yssem.at[group])
    for ph in range(2):
        left_here(pbuf.at[ph], mrs.at[ph, 0])
        left_here(bigf.at[ph, 0], mrs.at[ph, 1])
        left_here(ybuf.at[ph, pl.ds(0, N_Y - 1)], ars.at[2 * ph, 2])
    for q in range(4):
        left_here(rcv.at[q, pl.ds(0, N_DP - 1)], ars.at[q, 0])
        left_here(agb.at[q, pl.ds(0, N_DP - 1)], ars.at[q, 1])
    for k in range(CAP):
        left_here(a2s.at[k, pl.ds(0, N_DP - 1)], a2ss.at[k])
        pltpu.make_async_copy(a2s.at[k, dp], a2o.at[k, dp], lsem.at[k]).wait()


def layer_kernel(ranks, fills, pt, ct, wu, wd, qu, qd):
    feats, tokens = pt.shape
    tc = tokens // NC
    width, ff = wu.shape
    half = width // 2
    vm = pl.BlockSpec(memory_space=pltpu.VMEM)
    sm = pl.BlockSpec(memory_space=pltpu.SMEM)
    anywhere = pl.BlockSpec(memory_space=pl.ANY)
    shape = jax.ShapeDtypeStruct
    outs = [
        shape((CAP, N_DP, feats, BLOCK), BF16),
        shape((width, 4 * RANK), BF16),
        shape((ff, 4 * RANK), BF16),
        shape((N_DP, 128), jnp.int32),
        shape((RANK, ff), F32),
        shape((RANK, width), F32),
    ]
    dma = pltpu.SemaphoreType.DMA
    scratch = [
        pltpu.VMEM((NC, width, tc), BF16),
        pltpu.VMEM((NC, width, tc), BF16),
        pltpu.VMEM((NC, ff, tc), BF16),
        pltpu.VMEM((NC, ff, tc), BF16),
        pltpu.VMEM((width, ff), BF16),
        pltpu.VMEM((ff, width), BF16),
        pltpu.VMEM((RANK, ff), F32),
        pltpu.VMEM((RANK, width), F32),
        pltpu.VMEM((ff, width), BF16),
        pltpu.VMEM((width, ff), BF16),
        pltpu.VMEM((2 * RANK, ff), BF16),
        pltpu.VMEM((2 * RANK, width), BF16),
        pltpu.VMEM((2, 2, RANK, half), F32),
        pltpu.VMEM((2, RANK, ff), F32),
        pltpu.VMEM((2, RANK, half), F32),
        pltpu.VMEM((4, N_DP, 4, half), F32),
        pltpu.VMEM((4, N_DP, 4, half), F32),
        pltpu.VMEM((2, 4, half), F32),
        pltpu.VMEM((2, N_Y, 4, half), F32),
        pltpu.VMEM((4, N_DP, 4, half), F32),
        pltpu.VMEM((2, 2, RANK, half), F32),
        pltpu.VMEM((2, RANK, 2 * RANK), F32),
        pltpu.VMEM((N_MP, RANK // 2, 2 * RANK), F32),
        pltpu.VMEM((NC, 2, N_Y * feats, tc), BF16),
        pltpu.VMEM((NC, N_Y * feats, tc), BF16),
        pltpu.VMEM((NC, N_Y * feats, tc), BF16),
    ]
    scratch += [pltpu.VMEM((HALF, feats, tc), BF16) for _ in range(8)]
    scratch += [
        pltpu.VMEM((tokens // BLOCK, feats, BLOCK), BF16),
        pltpu.VMEM((CAP, N_DP, feats, BLOCK), BF16),
        pltpu.VMEM((width, 4 * RANK), BF16),
        pltpu.VMEM((ff, 4 * RANK), BF16),
        pltpu.VMEM((8, 128), jnp.int32),
        pltpu.VMEM((N_DP, 8, 128), jnp.int32),
        dma((6,)),
        dma((NC, 3)),
        dma((NC,)),
        dma((2,)),
        dma((NC,)),
        dma((1,)),
        dma((6,)),
        dma((6,)),
        dma((4, 3)),
        dma((4, 3)),
        dma((2, 2)),
        dma((2, 2)),
        dma((2,)),
        dma((2,)),
        dma((CAP,)),
        dma((CAP,)),
    ]
    return pl.pallas_call(
        kernel_body,
        out_shape=outs,
        in_specs=[sm] * 2 + [anywhere] * 6,
        out_specs=[anywhere] * 3 + [vm] * 3,
        scratch_shapes=scratch,
        compiler_params=pltpu.CompilerParams(
            collective_id=0, has_side_effects=True, vmem_limit_bytes=60 * 1024 * 1024
        ),
        name="layer",
    )(ranks, fills, pt, ct, wu, wd, qu, qd)


def finish_body(
    ranks, landed, a4u, a4d, qnu, qnd,
    enc, up, down, new_u, new_d,
    blocks, placed, ups, downs, b4u, b4d, origin, sems,
):
    me = lax.axis_index("dp")
    for k in range(CAP):
        pltpu.make_async_copy(landed.at[k], blocks.at[pl.ds(k * N_DP, N_DP)], sems.at[10 + k]).start()
    for slot in range(RMAX + 1):
        origin[slot] = CAP * N_DP
    filled = jnp.int32(0)
    for r in range(N_DP):
        seen = jnp.int32(0)
        for b in range(BLK_DEV):
            hit = (ranks[r, b] == me).astype(jnp.int32)
            held = origin[filled]
            origin[filled] = jnp.where(hit > 0, seen * N_DP + r, held)
            seen = seen + hit
            filled = filled + hit
    copies = []
    b4u[...] = right4(qnu[...])
    b4d[...] = right4(qnd[...])
    for k, (a, b, stage, out) in enumerate(((a4u, b4u, ups, up), (a4d, b4d, downs, down))):
        pieces = 2
        size = stage.shape[0] // pieces
        for j in range(pieces):
            at = pl.ds(j * size, size)
            stage[at, :] = mm(a[at, :], b[...])
            copy = pltpu.make_async_copy(stage.at[at, :], out.at[at, :], sems.at[k * pieces + j])
            copy.start()
            copies.append(copy)
    new_u[...] = qnu[...]
    new_d[...] = qnd[...]
    blocks[CAP * N_DP] = jnp.zeros_like(blocks[CAP * N_DP])
    for k in range(CAP):
        pltpu.make_async_copy(landed.at[k], blocks.at[pl.ds(k * N_DP, N_DP)], sems.at[10 + k]).wait()
    for slot in range(RMAX):
        placed[:, slot * BLOCK : (slot + 1) * BLOCK] = blocks[origin[slot]]
    copy = pltpu.make_async_copy(placed, enc, sems.at[12])
    copy.start()
    copies.append(copy)
    for copy in copies:
        copy.wait()


def finish(landed, a4u, a4d, ranks, qnu, qnd):
    feats = landed.shape[2]
    width, ff = a4u.shape[0], a4d.shape[0]
    vm = pl.BlockSpec(memory_space=pltpu.VMEM)
    anywhere = pl.BlockSpec(memory_space=pl.ANY)
    shape = jax.ShapeDtypeStruct
    return pl.pallas_call(
        finish_body,
        out_shape=[
            shape((feats, RMAX * BLOCK), BF16),
            shape((width, ff), F32),
            shape((ff, width), F32),
            shape(qnu.shape, F32),
            shape(qnd.shape, F32),
        ],
        in_specs=[pl.BlockSpec(memory_space=pltpu.SMEM), anywhere] + [vm] * 4,
        out_specs=[anywhere] * 3 + [vm] * 2,
        scratch_shapes=[
            pltpu.VMEM((CAP * N_DP + 1, *landed.shape[2:]), BF16),
            pltpu.VMEM((feats, RMAX * BLOCK), BF16),
            pltpu.VMEM((width, ff), F32),
            pltpu.VMEM((ff, width), F32),
            pltpu.VMEM((4 * RANK, ff), BF16),
            pltpu.VMEM((4 * RANK, width), BF16),
            pltpu.SMEM((RMAX + 1,), jnp.int32),
            pltpu.SemaphoreType.DMA((13,)),
        ],
        name="finish",
    )(ranks, landed, a4u, a4d, qnu, qnd)


def local(patches, cotangent, encoder_rank, block_fill, w_up, w_down, q_up, q_down):
    results = layer_kernel(
        encoder_rank, block_fill, patches.T, cotangent.T, w_up, w_down, q_up.T, q_down.T
    )
    encoded, approx_up, approx_down, new_u, new_d = finish(*results)
    return (encoded.T, approx_up, approx_down, new_u.T, new_d.T)


def solution(mesh):
    in_specs = (
        P("dp", "mp"), P("dp", "mp"), P("dp"), P("dp"), P(None, "mp"), P("mp", None), P("mp", None), P(),
    )
    out_specs = (P("dp", "mp"), P(None, "mp"), P("mp", None), P("mp", None), P())
    return jax.shard_map(local, mesh=mesh, in_specs=in_specs, out_specs=out_specs, check_vma=False)
```

time: 401 us -> 98.9 us (0.25)
  waiting for transfers between devices: 187 us -> 0 us
  Pallas kernels: 0 us -> 98.1 us
  blocking collectives: 53.4 us -> 0 us
  matrix products: 46.6 us -> 0 us
  other arithmetic: 35.9 us -> 0 us
  local copies, waits for them, and re-layouts: 33.2 us -> 0 us
  starting transfers between devices: 28.3 us -> 0 us
  between operations: 15.1 us -> 0.64 us
    psum x4 -> x0, waiting for transfers between devices: 104 us -> none  [over_axes(): shard = lax.psum(shard, axis)]
    pallas_call x0 -> x2, Pallas kernels: none -> 98.1 us  [the longest x1 92.4 us: layer_kernel(): pl.pallas_call(kernel_body, out_shape=outs, in_specs=[sm] * 2 + [anywhere...]
    all_gather x1 -> x0, waiting for transfers between devices: 51.1 us -> none  [rows_first(): whole, at, done = (lax.all_gather(both, axis, axis=0, tiled=True), 0, [])]
    dot_general x14 -> x0, matrix products: 44.2 us -> none  [the longest x1 11.1 us: local_layer(): lax.dot_general(patches_full, grad_pre, (((0,), (0,)), ((), ())), preferr...]
    all_gather x4 -> x0, blocking collectives: 33.4 us -> none  [all_blocks(): blocks = lax.all_gather(blocks, axes[k], axis=0, tiled=True)]
    all_to_all x5 -> x0, waiting for transfers between devices: 30.9 us -> none  [the longest x3 30.9 us: copy_for_each(): lax.all_to_all(jnp.broadcast_to(shard[None], (count, *shard.shape)), axis...]
    all_to_all x5 -> x0, starting transfers between devices: 27.4 us -> none  [the longest x3 17.8 us: copy_for_each(): lax.all_to_all(jnp.broadcast_to(shard[None], (count, *shard.shape)), axis...]
    another operation x11 -> x0, other arithmetic: 24.8 us -> none  [the longest x6 13 us: orthonormal(): lower = jnp.linalg.cholesky(gram)]
  transfers between devices with their start and end apart: 13 -> 0, of which waited for: 7 -> 0; matrix products, arithmetic and copies ran while one was open for 23% -> 0% of each run, Pallas kernels for 0% -> 0%
where the time goes in v2:
time: 98.9 us; the launch traced here: 98.7 us
  Pallas kernels  98.1 us (99%)
    pallas_call x1, Pallas kernels, layer_kernel(): pl.pallas_call(kernel_body, out_shape=outs, in_specs=[sm] * 2 + [anywhere...  92.4 us
    pallas_call x1, Pallas kernels, finish(): pl.pallas_call(finish_body, out_shape=[shape((feats, RMAX * BLOCK), BF16)...  5.72 us

profile of v2, /device:TPU:1, one launch (start us, length us, event | category | flops | bytes accessed | tf_op | source)
XLA Modules:
  0.0 98.7 jit_solution(11676064642856372309)
XLA Ops:
  0.6 92.4 %layer.1 = (bf16[2,16,160,128]{3,2,1,0:T(8,128)(2,1)}, bf16[1280,256]{1,0:T(8,128)(2,1)}, bf16[640,256]{1,0:T(8,128)(2,1)}, s32[16,128]{1,0:T(8,128)}, f32[64,640]{1,0:T(8,128)}, /*index=5*/f32[64,1280]{1,0:T(8,128)}) custom-call(s32[12]{0:T(128)} %ranks.1, s32[12]{0:T(128)} %fills.1, bf16[160,1536]{1,0:T(8,128)(2,1)} %bitcast.7, bf16[160,1536]{1,0:T(8,128)(2,1)} %bitcast.8, ...), custom_call_target="tpu_custom_call" | custom-call | tf_op jit(solution)/shard_map/layer/pallas_call | solution.py:564
  93.0 5.7 %finish.1 = (bf16[160,2304]{1,0:T(8,128)(2,1)}, f32[1280,640]{1,0:T(8,128)}, f32[640,1280]{1,0:T(8,128)}, f32[64,640]{1,0:T(8,128)}, f32[64,1280]{1,0:T(8,128)}) custom-call(s32[16,128]{1,0:T(8,128)} %get-tuple-element.16.ranks, bf16[2,16,160,128]{3,2,1,0:T(8,128)(2,1)} %get-tuple-element.17.landed, bf16[1280,256]{1,0:T(8,128)(2,1)} %get-tuple-element.18.a4u, ...), custom_call_target="tpu_custom_call" | custom-call | tf_op jit(solution)/shard_map/finish/pallas_call | solution.py:628

commit v3 on v2

--- a/solution.py
+++ b/solution.py
@@ -12,6 +12,7 @@
 N_DP = 16
 N_Y = 4
 N_MP = 8
+GROUPS = ((1, 4, 10, 15), (2, 8, 7, 13), (3, 12, 5, 11), (6, 9, 14))
 RANK = 64
 NC = 6
 HALF = NC // 2
@@ -125,7 +126,7 @@
         pltpu.make_async_copy(ref, ref, sem).wait()
 
     def dp_at(t):
-        return (dp + t) % N_DP
+        return ((dp // N_Y + t // N_Y) % N_Y) * N_Y + (dp + t) % N_Y
 
     def mp_at(t):
         return (mp + t) % N_MP
@@ -249,59 +250,6 @@
     def y_send(src, dst, group, to):
         send(src, dst, yssem.at[group], ysem.at[group], dp, to).start()
 
-    def step(i, carry):
-        @pl.when(i < NC)
-        def _():
-            arrived(pair(i), nsem.at[i, 0])
-            pass_on(xall, 0, i, left, right, nsem.at[i, 2])
-            pass_on(call, 1, i, right, left, nsem.at[i, 2])
-
-            @pl.when(i + AHEAD < NC)
-            def _():
-                start_own(i + AHEAD)
-
-            pass_on(xall, 0, i, left, mate, msem.at[i])
-            pass_on(call, 1, i, right, mate, msem.at[i])
-
-        @pl.when(i > 1)
-        def _():
-            arrived(xall.at[i - 2], msem.at[i - 2])
-            work_a(i - 2)
-
-        @pl.when(i < NC)
-        def _():
-            arrived(pair(i), nsem.at[i, 1])
-            pass_on(call, 1, i, left, mate, msem.at[i])
-            pass_on(xall, 0, i, right, mate, msem.at[i])
-
-        @pl.when(i > 1)
-        def _():
-            add_projection(i - 2)
-
-        @pl.when(jnp.logical_and(i > 2, i <= NC))
-        def _():
-            out_sum(i - 3)
-
-        @pl.when(i == NC)
-        def _():
-            y_send(piece(0, far), ra, 0, left)
-            y_send(piece(0, right), da, 4, right)
-            send_b(HALF)
-
-        @pl.when(jnp.logical_and(i > 0, i <= NC))
-        def _():
-            arrived(pair(i - 1), nsem.at[i - 1, 2])
-            pass_on(xall, 0, i - 1, far, mate, msem.at[i - 1])
-            pass_on(call, 1, i - 1, far, mate, msem.at[i - 1])
-
-        @pl.when(jnp.logical_and(i > 1, i < NC))
-        def _():
-            work_b(i - 2)
-
-        return carry
-
-    lax.fori_loop(0, NC + 2, step, 0)
-
     def mate_start(ph):
         send(proj.at[ph, 1 - c], pbuf.at[ph], mrs.at[ph, 0], mrr.at[ph, 0], dp, mate).start()
 
@@ -359,19 +307,76 @@
         arrived(bigf.at[ph, 0], mrr.at[ph, 1])
         return jnp.concatenate([bigf[ph, 0], bigf[ph, 1]], axis=1)
 
-    def start_slots(k, first, last):
-        for t in range(first, last):
+    def step(i, carry):
+        @pl.when(i < NC)
+        def _():
+            arrived(pair(i), nsem.at[i, 0])
+            pass_on(xall, 0, i, left, right, nsem.at[i, 2])
+            pass_on(call, 1, i, right, left, nsem.at[i, 2])
+
+            @pl.when(i + AHEAD < NC)
+            def _():
+                start_own(i + AHEAD)
+
+            pass_on(xall, 0, i, left, mate, msem.at[i])
+            pass_on(call, 1, i, right, mate, msem.at[i])
+
+        @pl.when(jnp.logical_and(i > 1, i < NC + 2))
+        def _():
+            arrived(xall.at[i - 2], msem.at[i - 2])
+            work_a(i - 2)
+
+        @pl.when(i < NC)
+        def _():
+            arrived(pair(i), nsem.at[i, 1])
+            pass_on(call, 1, i, left, mate, msem.at[i])
+            pass_on(xall, 0, i, right, mate, msem.at[i])
+
+        @pl.when(jnp.logical_and(i > 1, i < NC + 2))
+        def _():
+            add_projection(i - 2)
+
+        @pl.when(jnp.logical_and(i > 2, i <= NC))
+        def _():
+            out_sum(i - 3)
+
+        @pl.when(i == NC)
+        def _():
+            y_send(piece(0, far), ra, 0, left)
+            y_send(piece(0, right), da, 4, right)
+            send_b(HALF)
+
+        @pl.when(jnp.logical_and(i > 0, i <= NC))
+        def _():
+            arrived(pair(i - 1), nsem.at[i - 1, 2])
+            pass_on(xall, 0, i - 1, far, mate, msem.at[i - 1])
+            pass_on(call, 1, i - 1, far, mate, msem.at[i - 1])
+
+        @pl.when(i == NC + 3)
+        def _():
+            scatter(0, mate_end(0))
+
+        @pl.when(jnp.logical_or(jnp.logical_and(i > 1, i < NC), i > NC + 1))
+        def _():
+            work_b(jnp.where(i < NC, i - 2, i - 4))
+
+        @pl.when(i == NC + 1)
+        def _():
+            mate_start(0)
+            scatter(1, small[0])
+
+        return carry
+
+    lax.fori_loop(0, NC + 4, step, 0)
+
+    def start_slots(k, group):
+        for t in GROUPS[group]:
             to = dp_at(t)
             send(a2s.at[k, to], a2o.at[k, dp], a2ss.at[k], a2rr.at[k], to, mp).start()
 
     def out_landed(k):
         arrived(a2o.at[k, pl.ds(0, N_DP - 1)], a2rr.at[k])
 
-    mate_start(0)
-    scatter(1, small[0])
-    work_b(NC - 2)
-    scatter(0, mate_end(0))
-    work_b(NC - 1)
     for i in range(HALF + 1, NC):
         out_sum(i)
         send_b(i)
@@ -381,11 +386,11 @@
     spread(1, collect(1))
     y_start(0, 0, collect(0))
     y_send(fa, ea, 2, left)
-    spread(0, y_end(0, 0))
     arrived(rb, ysem.at[1])
     for i in range(HALF):
         fb[i] = (own_rows(HALF + i, right).astype(F32) + rb[i].astype(F32)).astype(BF16)
     y_send(fb, eb, 3, right)
+    spread(0, y_end(0, 0))
     proj_down = small_end(0, 1)
     quh[:, :half] = stack2(proj_down)
 
@@ -401,14 +406,6 @@
         send(gbuf.at[mp], gbuf.at[mp], xs.at[1], xr.at[1], dp, mp_at(t)).start()
     big_start(0, 0)
     scatter(2, mate_end(1))
-    proj_up = big_end(0)
-    qdh[...] = stack2(proj_up)
-
-    def fresh_up(i, carry):
-        small_add(1, fold2(mm(qdh[...], xall[i])), gp[i])
-        return carry
-
-    lax.fori_loop(0, HALF, fresh_up, 0)
     arrived(ea, ysem.at[2])
     arrived(eb, ysem.at[3])
     arrived(da, ysem.at[4])
@@ -429,12 +426,22 @@
             first = jnp.where(here, b, first)
         a2s[0, j] = ob[first]
         a2s[1, j] = ob[second]
-    start_slots(0, 1, 8)
+    start_slots(0, 0)
+    start_slots(0, 1)
     for k in range(CAP):
         pltpu.make_async_copy(a2s.at[k, dp], a2o.at[k, dp], lsem.at[k]).start()
-    lax.fori_loop(HALF, NC, fresh_up, 0)
+    proj_up = big_end(0)
+    qdh[...] = stack2(proj_up)
+
+    def fresh_up(i, carry):
+        small_add(1, fold2(mm(qdh[...], xall[i])), gp[i])
+        return carry
+
+
+    lax.fori_loop(0, NC, fresh_up, 0)
     scatter(3, small[1])
-    start_slots(0, 8, N_DP)
+    start_slots(0, 2)
+    start_slots(0, 3)
     y_start(1, 2, collect(2))
     elim[0] = identity_at_right((RANK, 2 * RANK))
     elim[0, :, :RANK] = gram_of(proj_up)
@@ -447,10 +454,12 @@
     elim[1, RANK // 2 :, :RANK] = gram_d[:, RANK:]
     elim[...] = eliminate(elim[...], 0, 8)
     spread(2, y_end(1, 2))
-    start_slots(1, 1, 8)
+    start_slots(1, 0)
     elim[...] = eliminate(elim[...], 8, 24)
     spread(3, collect(3))
-    start_slots(1, 8, N_DP)
+    start_slots(1, 1)
+    start_slots(1, 2)
+    start_slots(1, 3)
     elim[...] = eliminate(elim[...], 24, RANK - 1)
     inv_u = left4(inverse_of_factor(elim[0]).T)
     inv_d = left4(inverse_of_factor(elim[1]).T)
@@ -582,17 +591,6 @@
     me = lax.axis_index("dp")
     for k in range(CAP):
         pltpu.make_async_copy(landed.at[k], blocks.at[pl.ds(k * N_DP, N_DP)], sems.at[10 + k]).start()
-    for slot in range(RMAX + 1):
-        origin[slot] = CAP * N_DP
-    filled = jnp.int32(0)
-    for r in range(N_DP):
-        seen = jnp.int32(0)
-        for b in range(BLK_DEV):
-            hit = (ranks[r, b] == me).astype(jnp.int32)
-            held = origin[filled]
-            origin[filled] = jnp.where(hit > 0, seen * N_DP + r, held)
-            seen = seen + hit
-            filled = filled + hit
     copies = []
     b4u[...] = right4(qnu[...])
     b4d[...] = right4(qnd[...])
@@ -607,6 +605,17 @@
             copies.append(copy)
     new_u[...] = qnu[...]
     new_d[...] = qnd[...]
+    for slot in range(RMAX + 1):
+        origin[slot] = CAP * N_DP
+    filled = jnp.int32(0)
+    for r in range(N_DP):
+        seen = jnp.int32(0)
+        for b in range(BLK_DEV):
+            hit = (ranks[r, b] == me).astype(jnp.int32)
+            held = origin[filled]
+            origin[filled] = jnp.where(hit > 0, seen * N_DP + r, held)
+            seen = seen + hit
+            filled = filled + hit
     blocks[CAP * N_DP] = jnp.zeros_like(blocks[CAP * N_DP])
     for k in range(CAP):
         pltpu.make_async_copy(landed.at[k], blocks.at[pl.ds(k * N_DP, N_DP)], sems.at[10 + k]).wait()

time: 98.9 us -> 96.3 us (0.974)
  Pallas kernels: 98.1 us -> 95.2 us
    pallas_call x1, Pallas kernels: 92.4 us -> 89.5 us  [layer_kernel(): pl.pallas_call(kernel_body, out_shape=outs, in_specs=[sm] * 2 + [anywhere...]
where the time goes in v3:
time: 96.3 us; the launch traced here: 95.9 us
  Pallas kernels  95.2 us (99%)
    pallas_call x1, Pallas kernels, layer_kernel(): pl.pallas_call(kernel_body, out_shape=outs, in_specs=[sm] * 2 + [anywhere...  89.5 us
    pallas_call x1, Pallas kernels, finish(): pl.pallas_call(finish_body, out_shape=[shape((feats, RMAX * BLOCK), BF16)...  5.72 us

profile of v3, /device:TPU:1, one launch (start us, length us, event | category | flops | bytes accessed | tf_op | source)
XLA Modules:
  0.0 95.9 jit_solution(7690175536256702421)
XLA Ops:
  0.6 89.5 %layer.1 = (bf16[2,16,160,128]{3,2,1,0:T(8,128)(2,1)}, bf16[1280,256]{1,0:T(8,128)(2,1)}, bf16[640,256]{1,0:T(8,128)(2,1)}, s32[16,128]{1,0:T(8,128)}, f32[64,640]{1,0:T(8,128)}, /*index=5*/f32[64,1280]{1,0:T(8,128)}) custom-call(s32[12]{0:T(128)} %ranks.1, s32[12]{0:T(128)} %fills.1, bf16[160,1536]{1,0:T(8,128)(2,1)} %bitcast.7, bf16[160,1536]{1,0:T(8,128)(2,1)} %bitcast.8, ...), custom_call_target="tpu_custom_call" | custom-call | tf_op jit(solution)/shard_map/layer/pallas_call | solution.py:573
  90.1 5.7 %finish.1 = (bf16[160,2304]{1,0:T(8,128)(2,1)}, f32[1280,640]{1,0:T(8,128)}, f32[640,1280]{1,0:T(8,128)}, f32[64,640]{1,0:T(8,128)}, f32[64,1280]{1,0:T(8,128)}) custom-call(s32[16,128]{1,0:T(8,128)} %get-tuple-element.16.ranks, bf16[2,16,160,128]{3,2,1,0:T(8,128)(2,1)} %get-tuple-element.17.landed, bf16[1280,256]{1,0:T(8,128)(2,1)} %get-tuple-element.18.a4u, ...), custom_call_target="tpu_custom_call" | custom-call | tf_op jit(solution)/shard_map/finish/pallas_call | solution.py:637

commit v4 on v3

--- a/solution.py
+++ b/solution.py
@@ -140,19 +140,15 @@
     for t in range(1, N_MP):
         pl.semaphore_signal(barrier, inc=1, device_id=(dp, mp_at(t)), device_id_type=MESH)
 
+    def fetch(src, dst, i, sem):
+        pltpu.make_async_copy(src.at[:, pl.ds(i * tc, tc)], rows(dst, i, mp), lsem.at[sem]).start()
+
     for i in range(NC):
-        pltpu.make_async_copy(ct.at[:, pl.ds(i * tc, tc)], rows(call, i, mp), lsem.at[0]).start()
-    for i in range(NC):
-        pltpu.make_async_copy(pt.at[:, pl.ds(i * tc, tc)], rows(xall, i, mp), lsem.at[1]).start()
+        fetch(ct, call, i, 0 if i < AHEAD else 6)
+        fetch(pt, xall, i, 1 if i < AHEAD else 7)
     weights = ((wu, wus), (wd, wds), (qu, qus), (qd, qds))
     for k, (src, dst) in enumerate(weights):
         pltpu.make_async_copy(src, dst, lsem.at[2 + k]).start()
-    lane8 = lax.broadcasted_iota(jnp.int32, (8, 128), 1)
-    mine = jnp.zeros((8, 128), jnp.int32)
-    for b in range(blocks):
-        mine = jnp.where(lane8 == b, ranks[b], mine)
-    ers[...] = mine
-    erb[dp] = mine
     token = lax.broadcasted_iota(jnp.int32, (feats, BLOCK), 1)
     def mask_cot(i):
         place_at = pl.ds(pl.multiple_of(mp * feats, 32), feats)
@@ -161,10 +157,10 @@
             kept = jnp.where(token < fills[i * per + k], call[i, place_at, lanes].astype(F32), 0.0)
             call[i, place_at, lanes] = kept.astype(BF16)
 
-    fetched(call.at[0, pl.ds(0, NC * feats), :], lsem.at[0])
+    fetched(call.at[0, pl.ds(0, AHEAD * feats), :], lsem.at[0])
     for i in range(AHEAD):
         mask_cot(i)
-    fetched(xall.at[0, pl.ds(0, NC * feats), :], lsem.at[1])
+    fetched(xall.at[0, pl.ds(0, AHEAD * feats), :], lsem.at[1])
     pl.semaphore_wait(barrier, N_DP + N_MP - 2)
 
     def pass_on(ref, which, i, owner, to, rsem):
@@ -181,11 +177,19 @@
 
     for i in range(AHEAD):
         start_own(i)
+    fetched(call.at[0, pl.ds(0, (NC - AHEAD) * feats), :], lsem.at[6])
+    fetched(xall.at[0, pl.ds(0, (NC - AHEAD) * feats), :], lsem.at[7])
     for i in range(AHEAD, NC):
         mask_cot(i)
     for i in range(NC):
         pass_on(xall, 0, i, mp, mate, msem.at[i])
         pass_on(call, 1, i, mp, mate, msem.at[i])
+    lane8 = lax.broadcasted_iota(jnp.int32, (8, 128), 1)
+    mine = jnp.zeros((8, 128), jnp.int32)
+    for b in range(blocks):
+        mine = jnp.where(lane8 == b, ranks[b], mine)
+    ers[...] = mine
+    erb[dp] = mine
     for t in range(1, N_DP):
         send(ers, erb.at[dp], xs.at[0], xr.at[0], dp_at(t), mp).start()
 
@@ -242,6 +246,9 @@
     def own_rows(i, owner):
         return osb[i, pl.ds(pl.multiple_of((owner // 2) * feats, 32), feats), :]
 
+    def send_a(j):
+        y_send(osb.at[j, pl.ds(pl.multiple_of((right // 2) * feats, 32), feats), :], da.at[j], 4, right)
+
     def send_b(i):
         j = i - HALF
         y_send(osb.at[i, pl.ds(pl.multiple_of((far // 2) * feats, 32), feats), :], rb.at[j], 1, right)
@@ -343,8 +350,9 @@
         @pl.when(i == NC)
         def _():
             y_send(piece(0, far), ra, 0, left)
-            y_send(piece(0, right), da, 4, right)
             send_b(HALF)
+            for j in range(HALF - 1):
+                send_a(j)
 
         @pl.when(jnp.logical_and(i > 0, i <= NC))
         def _():
@@ -380,6 +388,7 @@
     for i in range(HALF + 1, NC):
         out_sum(i)
         send_b(i)
+    send_a(HALF - 1)
     arrived(ra, ysem.at[0])
     for i in range(HALF):
         fa[i] = (own_rows(i, left).astype(F32) + ra[i].astype(F32)).astype(BF16)
@@ -398,7 +407,7 @@
         big_add(1, fold2(mm(quh[...], hid[i])), call[i])
         return carry
 
-    lax.fori_loop(0, NC, fresh_down, 0)
+    lax.fori_loop(0, NC, fresh_down, 0, unroll=2)
     mate_start(1)
     gram_d = gram_of(proj_down)
     gbuf[mp] = jnp.concatenate([gram_d[: RANK // 2], gram_d[RANK // 2 :]], axis=1)
@@ -438,7 +447,7 @@
         return carry
 
 
-    lax.fori_loop(0, NC, fresh_up, 0)
+    lax.fori_loop(0, NC, fresh_up, 0, unroll=2)
     scatter(3, small[1])
     start_slots(0, 2)
     start_slots(0, 3)
@@ -553,7 +562,7 @@
         pltpu.VMEM((ff, 4 * RANK), BF16),
         pltpu.VMEM((8, 128), jnp.int32),
         pltpu.VMEM((N_DP, 8, 128), jnp.int32),
-        dma((6,)),
+        dma((8,)),
         dma((NC, 3)),
         dma((NC,)),
         dma((2,)),

time: 96.3 us -> 96.1 us (level)
  no operation moved by 1% of the time
where the time goes in v4:
time: 96.1 us; the launch traced here: 95.7 us
  Pallas kernels  95.1 us (99%)
    pallas_call x1, Pallas kernels, layer_kernel(): pl.pallas_call(kernel_body, out_shape=outs, in_specs=[sm] * 2 + [anywhere...  89.3 us
    pallas_call x1, Pallas kernels, finish(): pl.pallas_call(finish_body, out_shape=[shape((feats, RMAX * BLOCK), BF16)...  5.72 us

profile of v4, /device:TPU:1, one launch (start us, length us, event | category | flops | bytes accessed | tf_op | source)
XLA Modules:
  0.0 95.7 jit_solution(1090623439349562202)
XLA Ops:
  0.6 89.3 %layer.1 = (bf16[2,16,160,128]{3,2,1,0:T(8,128)(2,1)}, bf16[1280,256]{1,0:T(8,128)(2,1)}, bf16[640,256]{1,0:T(8,128)(2,1)}, s32[16,128]{1,0:T(8,128)}, f32[64,640]{1,0:T(8,128)}, /*index=5*/f32[64,1280]{1,0:T(8,128)}) custom-call(s32[12]{0:T(128)} %ranks.1, s32[12]{0:T(128)} %fills.1, bf16[160,1536]{1,0:T(8,128)(2,1)} %bitcast.7, bf16[160,1536]{1,0:T(8,128)(2,1)} %bitcast.8, ...), custom_call_target="tpu_custom_call" | custom-call | tf_op jit(solution)/shard_map/layer/pallas_call | solution.py:582
  90.0 5.7 %finish.1 = (bf16[160,2304]{1,0:T(8,128)(2,1)}, f32[1280,640]{1,0:T(8,128)}, f32[640,1280]{1,0:T(8,128)}, f32[64,640]{1,0:T(8,128)}, f32[64,1280]{1,0:T(8,128)}) custom-call(s32[16,128]{1,0:T(8,128)} %get-tuple-element.16.ranks, bf16[2,16,160,128]{3,2,1,0:T(8,128)(2,1)} %get-tuple-element.17.landed, bf16[1280,256]{1,0:T(8,128)(2,1)} %get-tuple-element.18.a4u, ...), custom_call_target="tpu_custom_call" | custom-call | tf_op jit(solution)/shard_map/finish/pallas_call | solution.py:646

commit v5 on v4

--- a/solution.py
+++ b/solution.py
@@ -93,7 +93,7 @@
     a2o, a4u, a4d, era_out, qnu, qnd,
     xall, call, hid, gp, wus, wds, qus, qds, wut, wdt, quh, qdh,
     proj, small, pbuf, rsb, rcv, ysend, ybuf, agb, bigf, elim,
-    gbuf, outp, po, osb, ra, rb, da, db, fa, fb, ea, eb, ob, a2s, f4u, f4d, ers, erb,
+    gbuf, outp, po, osb, ra, rb, da, db, fa, fb, ea, eb, ob, a2s, f4u, f4d, fu, fd, ef, ers, erb,
     lsem, nsem, msem, gsem, osem, ossem, ysem, yssem, arr, ars, mrr, mrs, xr, xs, a2rr, a2ss,
 ):
     dp = lax.axis_index("dp")
@@ -461,12 +461,12 @@
     elim[1] = identity_at_right((RANK, 2 * RANK))
     elim[1, : RANK // 2, :RANK] = gram_d[:, :RANK]
     elim[1, RANK // 2 :, :RANK] = gram_d[:, RANK:]
+    start_slots(1, 0)
     elim[...] = eliminate(elim[...], 0, 8)
     spread(2, y_end(1, 2))
-    start_slots(1, 0)
+    start_slots(1, 1)
     elim[...] = eliminate(elim[...], 8, 24)
     spread(3, collect(3))
-    start_slots(1, 1)
     start_slots(1, 2)
     start_slots(1, 3)
     elim[...] = eliminate(elim[...], 24, RANK - 1)
@@ -478,17 +478,23 @@
     pltpu.make_async_copy(f4d, a4d, lsem.at[3]).start()
     arrived(erb.at[pl.ds(0, N_DP - 1)], xr.at[0])
     for r in range(N_DP):
-        era_out[r : r + 1, :] = erb[r, 0:1, :]
+        ef[r : r + 1, :] = erb[r, 0:1, :]
+    pltpu.make_async_copy(ef, era_out, lsem.at[4]).start()
     big_start(1, 2)
     out_landed(0)
     new_u = mm_tn(inv_u, right4(small_end(1, 3)))
-    qnu[...] = new_u
+    fu[...] = new_u
+    pltpu.make_async_copy(fu, qnu, lsem.at[5]).start()
     new_d = mm_tn(inv_d, right4(big_end(1)))
-    qnd[...] = new_d
+    fd[...] = new_d
+    pltpu.make_async_copy(fd, qnd, lsem.at[6]).start()
     out_landed(1)
 
     pltpu.make_async_copy(f4u, a4u, lsem.at[2]).wait()
     pltpu.make_async_copy(f4d, a4d, lsem.at[3]).wait()
+    pltpu.make_async_copy(ef, era_out, lsem.at[4]).wait()
+    pltpu.make_async_copy(fu, qnu, lsem.at[5]).wait()
+    pltpu.make_async_copy(fd, qnd, lsem.at[6]).wait()
     left_here(xall.at[:, pl.ds(0, 7 * feats), :], gsem.at[0])
     left_here(call.at[:, pl.ds(0, 7 * feats), :], gsem.at[1])
     left_here(po, ossem.at[0])
@@ -513,7 +519,6 @@
     tc = tokens // NC
     width, ff = wu.shape
     half = width // 2
-    vm = pl.BlockSpec(memory_space=pltpu.VMEM)
     sm = pl.BlockSpec(memory_space=pltpu.SMEM)
     anywhere = pl.BlockSpec(memory_space=pl.ANY)
     shape = jax.ShapeDtypeStruct
@@ -560,6 +565,9 @@
         pltpu.VMEM((CAP, N_DP, feats, BLOCK), BF16),
         pltpu.VMEM((width, 4 * RANK), BF16),
         pltpu.VMEM((ff, 4 * RANK), BF16),
+        pltpu.VMEM((RANK, ff), F32),
+        pltpu.VMEM((RANK, width), F32),
+        pltpu.VMEM((N_DP, 128), jnp.int32),
         pltpu.VMEM((8, 128), jnp.int32),
         pltpu.VMEM((N_DP, 8, 128), jnp.int32),
         dma((8,)),
@@ -583,7 +591,7 @@
         kernel_body,
         out_shape=outs,
         in_specs=[sm] * 2 + [anywhere] * 6,
-        out_specs=[anywhere] * 3 + [vm] * 3,
+        out_specs=[anywhere] * len(outs),
         scratch_shapes=scratch,
         compiler_params=pltpu.CompilerParams(
             collective_id=0, has_side_effects=True, vmem_limit_bytes=60 * 1024 * 1024

time: 96.1 us -> 95.2 us (level)
  no operation moved by 1% of the time
where the time goes in v5:
time: 95.2 us; the launch traced here: 95 us
  Pallas kernels  94.4 us (99%)
    pallas_call x1, Pallas kernels, layer_kernel(): pl.pallas_call(kernel_body, out_shape=outs, in_specs=[sm] * 2 + [anywhere...  88.7 us
    pallas_call x1, Pallas kernels, finish(): pl.pallas_call(finish_body, out_shape=[shape((feats, RMAX * BLOCK), BF16)...  5.72 us

profile of v5, /device:TPU:1, one launch (start us, length us, event | category | flops | bytes accessed | tf_op | source)
XLA Modules:
  0.0 95.0 jit_solution(16295176191465774933)
XLA Ops:
  0.6 88.7 %layer.1 = (bf16[2,16,160,128]{3,2,1,0:T(8,128)(2,1)}, bf16[1280,256]{1,0:T(8,128)(2,1)}, bf16[640,256]{1,0:T(8,128)(2,1)}, s32[16,128]{1,0:T(8,128)}, f32[64,640]{1,0:T(8,128)}, /*index=5*/f32[64,1280]{1,0:T(8,128)}) custom-call(s32[12]{0:T(128)} %ranks.1, s32[12]{0:T(128)} %fills.1, bf16[160,1536]{1,0:T(8,128)(2,1)} %bitcast.7, bf16[160,1536]{1,0:T(8,128)(2,1)} %bitcast.8, ...), custom_call_target="tpu_custom_call" | custom-call | tf_op jit(solution)/shard_map/layer/pallas_call | solution.py:590
  89.3 5.7 %finish.1 = (bf16[160,2304]{1,0:T(8,128)(2,1)}, f32[1280,640]{1,0:T(8,128)}, f32[640,1280]{1,0:T(8,128)}, f32[64,640]{1,0:T(8,128)}, f32[64,1280]{1,0:T(8,128)}) custom-call(s32[16,128]{1,0:T(8,128)} %get-tuple-element.16.ranks, bf16[2,16,160,128]{3,2,1,0:T(8,128)(2,1)} %get-tuple-element.17.landed, bf16[1280,256]{1,0:T(8,128)(2,1)} %get-tuple-element.18.a4u, ...), custom_call_target="tpu_custom_call" | custom-call | tf_op jit(solution)/shard_map/finish/pallas_call | solution.py:654

commit v6 on v5

--- a/solution.py
+++ b/solution.py
@@ -609,6 +609,10 @@
     for k in range(CAP):
         pltpu.make_async_copy(landed.at[k], blocks.at[pl.ds(k * N_DP, N_DP)], sems.at[10 + k]).start()
     copies = []
+    for k, (src, dst) in enumerate(((qnu, new_u), (qnd, new_d))):
+        copy = pltpu.make_async_copy(src, dst, sems.at[13 + k])
+        copy.start()
+        copies.append(copy)
     b4u[...] = right4(qnu[...])
     b4d[...] = right4(qnd[...])
     for k, (a, b, stage, out) in enumerate(((a4u, b4u, ups, up), (a4d, b4d, downs, down))):
@@ -620,8 +624,6 @@
             copy = pltpu.make_async_copy(stage.at[at, :], out.at[at, :], sems.at[k * pieces + j])
             copy.start()
             copies.append(copy)
-    new_u[...] = qnu[...]
-    new_d[...] = qnd[...]
     for slot in range(RMAX + 1):
         origin[slot] = CAP * N_DP
     filled = jnp.int32(0)
@@ -661,7 +663,7 @@
             shape(qnd.shape, F32),
         ],
         in_specs=[pl.BlockSpec(memory_space=pltpu.SMEM), anywhere] + [vm] * 4,
-        out_specs=[anywhere] * 3 + [vm] * 2,
+        out_specs=[anywhere] * 5,
         scratch_shapes=[
             pltpu.VMEM((CAP * N_DP + 1, *landed.shape[2:]), BF16),
             pltpu.VMEM((feats, RMAX * BLOCK), BF16),
@@ -670,7 +672,7 @@
             pltpu.VMEM((4 * RANK, ff), BF16),
             pltpu.VMEM((4 * RANK, width), BF16),
             pltpu.SMEM((RMAX + 1,), jnp.int32),
-            pltpu.SemaphoreType.DMA((13,)),
+            pltpu.SemaphoreType.DMA((15,)),
         ],
         name="finish",
     )(ranks, landed, a4u, a4d, qnu, qnd)

time: 95.2 us -> 94.5 us (level)
  no operation moved by 1% of the time
where the time goes in v6:
time: 94.5 us; the launch traced here: 94.3 us
  Pallas kernels  93.6 us (99%)
    pallas_call x1, Pallas kernels, layer_kernel(): pl.pallas_call(kernel_body, out_shape=outs, in_specs=[sm] * 2 + [anywhere...  88.7 us
    pallas_call x1, Pallas kernels, finish(): pl.pallas_call(finish_body, out_shape=[shape((feats, RMAX * BLOCK), BF16)...  4.97 us

profile of v6, /device:TPU:1, one launch (start us, length us, event | category | flops | bytes accessed | tf_op | source)
XLA Modules:
  0.0 94.3 jit_solution(3180693893684501898)
XLA Ops:
  0.6 88.7 %layer.1 = (bf16[2,16,160,128]{3,2,1,0:T(8,128)(2,1)}, bf16[1280,256]{1,0:T(8,128)(2,1)}, bf16[640,256]{1,0:T(8,128)(2,1)}, s32[16,128]{1,0:T(8,128)}, f32[64,640]{1,0:T(8,128)}, /*index=5*/f32[64,1280]{1,0:T(8,128)}) custom-call(s32[12]{0:T(128)} %ranks.1, s32[12]{0:T(128)} %fills.1, bf16[160,1536]{1,0:T(8,128)(2,1)} %bitcast.7, bf16[160,1536]{1,0:T(8,128)(2,1)} %bitcast.8, ...), custom_call_target="tpu_custom_call" | custom-call | tf_op jit(solution)/shard_map/layer/pallas_call | solution.py:590
  89.3 5.0 %finish.1 = (bf16[160,2304]{1,0:T(8,128)(2,1)}, f32[1280,640]{1,0:T(8,128)}, f32[640,1280]{1,0:T(8,128)}, f32[64,640]{1,0:T(8,128)}, f32[64,1280]{1,0:T(8,128)}) custom-call(s32[16,128]{1,0:T(8,128)} %get-tuple-element.16.ranks, bf16[2,16,160,128]{3,2,1,0:T(8,128)(2,1)} %get-tuple-element.17.landed, bf16[1280,256]{1,0:T(8,128)(2,1)} %get-tuple-element.18.a4u, ...), custom_call_target="tpu_custom_call" | custom-call | tf_op jit(solution)/shard_map/finish/pallas_call | solution.py:656
